TPU v7x, 256 devices: a whole 4x4x8 slice. The times are simulated.
256 devices in a mesh: gx: 16 (over z_hi, x), gy: 4 (over y), gz: 4 (over z_lo, core).
Axes of the slice: x: 4, y: 4, z: 8 (z_hi: 4, z_lo: 2; z = z_hi * 2 + z_lo), core: 2. Of those that a mesh axis runs over, the one named last changes fastest.
Arguments:
- ambient_motion_array: float32 [3, 128, 256, 512], P(None, 'gx', 'gy', 'gz'), may hold values from -6 to 6
- ambient_scalar_trio: float32 [3, 128, 256, 512], P(None, 'gx', 'gy', 'gz'), may hold values from 0.2 to 1
- droplet_local_position: float32 [3, 262144], P(None, ('gx', 'gy', 'gz')), may hold values from -0.5 to 0.5
- droplet_motion_array: float32 [3, 262144], P(None, ('gx', 'gy', 'gz')), may hold values from -6 to 6
- droplet_heat_level: float32 [262144], P(('gx', 'gy', 'gz')), may hold values from 0.3 to 0.9
- droplet_size_quadratic: float32 [262144], P(('gx', 'gy', 'gz')), may hold values from 0.25 to 4
- local_i_position: int32 [262144], P(('gx', 'gy', 'gz')), may hold values from 0 to 7
- local_j_position: int32 [262144], P(('gx', 'gy', 'gz')), may hold values from 0 to 63
- local_k_position: int32 [262144], P(('gx', 'gy', 'gz')), may hold values from 0 to 127
- active_group_tally: int32 [256], P(('gx', 'gy', 'gz')), may hold values from 1 to 8, as said below
Outputs:
- gas_source: float32 [5, 128, 256, 512], P(None, 'gx', 'gy', 'gz')
- parcel_state: float32 [5, 262144], P(None, ('gx', 'gy', 'gz'))
Inputs may be any that keep to these rules, and one draw needn't show every extreme that they name: `active_group_tally`: tiles of a brick are live from the first one on; in every draw some brick has all 8 tiles live.
All inputs are finite; a program needn't handle non-finite values.
Results may differ from a plain program's by a relative error of at most 0.0003.
Values sent between devices are 32-bit elements; how exact they have to be, the bound alone decides.
A program may use at most 128 MiB of HBM per device.

v0:
```python
import functools

import jax
import jax.numpy as jnp
from jax import lax
from jax.experimental import pallas as pl
from jax.experimental.pallas import tpu as pltpu
from jax.sharding import PartitionSpec as P

TILE = 128
NF = 6
NS = 5
CI, CJ, CK = 8, 64, 128
OWN = CI * CJ
XB = OWN
YB = OWN + 128
COLS = OWN + 256
ROWS = NF * CK + 16
MESH = pl.DeviceIdType.MESH
F32 = jnp.float32
BF16 = jnp.bfloat16

step_time = 0.25
evap_rate = 1.0
heat_rate = 2.0
boiling_energy_drain = 0.3


def split(x):
    hi = x.astype(BF16)
    return hi, (x - hi.astype(F32)).astype(BF16)


def tent(offset):
    return jnp.maximum(0.0, 1.0 - jnp.abs(offset))


def iota(shape, dim):
    return lax.broadcasted_iota(jnp.int32, shape, dim)


def kernel(
    sizes,
    vel,
    scal,
    pos,
    mot,
    heat,
    diam,
    li,
    lj,
    lk,
    tally,
    out,
    state,
    fields,
    a_hi,
    a_lo,
    s_hi,
    s_lo,
    t_hi,
    t_lo,
    picked,
    wi,
    lines,
    line_ends,
    gathered,
    xb,
    yb,
    y_out,
    z_out,
    z_in,
    xz_out,
    xz_in,
    xy_out,
    xy_in,
    dx_out,
    dx_in,
    dy,
    dy_in,
    dz_out,
    dz_in,
    dxe_out,
    dxe_in,
    local_sem,
    send_sem,
    recv_sem,
):
    n = pos.shape[1]
    me = {axis: lax.axis_index(axis) for axis in sizes}
    ends = {axis: size - 1 for axis, size in sizes.items()}

    def copy(src, dst, number, side, axis, peer):
        return pltpu.make_async_remote_copy(
            src_ref=src,
            dst_ref=dst,
            send_sem=send_sem.at[2 * number + side],
            recv_sem=recv_sem.at[2 * number + side],
            device_id={axis: peer},
            device_id_type=MESH,
        )

    def send(number, axis, up, land0, down, land1):
        @pl.when(me[axis] < ends[axis])
        def _():
            copy(up, land0, number, 0, axis, me[axis] + 1).start()

        @pl.when(me[axis] > 0)
        def _():
            copy(down, land1, number, 1, axis, me[axis] - 1).start()

    def arrive(number, axis, up, land0, down, land1):
        @pl.when(me[axis] > 0)
        def _():
            copy(up, land0, number, 0, axis, me[axis] - 1).wait_recv()

        @pl.when(me[axis] < ends[axis])
        def _():
            copy(down, land1, number, 1, axis, me[axis] + 1).wait_recv()

    def sent(number, axis, up, land0, down, land1):
        @pl.when(me[axis] < ends[axis])
        def _():
            copy(up, land0, number, 0, axis, me[axis] + 1).wait_send()

        @pl.when(me[axis] > 0)
        def _():
            copy(down, land1, number, 1, axis, me[axis] - 1).wait_send()

    def blank(axis, land0, land1):
        @pl.when(me[axis] == 0)
        def _():
            land0[...] = jnp.zeros(land0.shape, F32)

        @pl.when(me[axis] == ends[axis])
        def _():
            land1[...] = jnp.zeros(land1.shape, F32)

    x_vel = (0, "gx", vel.at[:, CI - 1], xb.at[0:3, 0:CJ], vel.at[:, 0], xb.at[0:3, CJ:128])
    x_scal = (1, "gx", scal.at[:, CI - 1], xb.at[3:6, 0:CJ], scal.at[:, 0], xb.at[3:6, CJ:128])
    y_rows = (2, "gy", y_out.at[1], yb.at[:, 0:8], y_out.at[0], yb.at[:, 16:24])
    z_cols = (3, "gz", z_out.at[1], z_in.at[0:8], z_out.at[0], z_in.at[8:16])
    xz_cols = (4, "gx", xz_out.at[1], xz_in.at[0], xz_out.at[0], xz_in.at[1])
    xy_rows = (5, "gx", xy_out.at[1], xy_in.at[0], xy_out.at[0], xy_in.at[1])
    d_x = (6, "gx", dx_out.at[1], dx_in.at[0], dx_out.at[0], dx_in.at[1])
    d_z = (7, "gz", dz_out.at[8:16], dz_in.at[0:8], dz_out.at[0:8], dz_in.at[8:16])
    d_y = (8, "gy", dy.at[16:32], dy_in.at[0], dy.at[0:16], dy_in.at[1])
    d_xe = (9, "gx", dxe_out.at[1], dxe_in.at[0], dxe_out.at[0], dxe_in.at[1])
    transfers = (x_vel, x_scal, y_rows, z_cols, xz_cols, xy_rows, d_x, d_z, d_y, d_xe)

    load_vel = pltpu.make_async_copy(vel, fields.at[0:3], local_sem.at[0])
    load_scal = pltpu.make_async_copy(scal, fields.at[3:6], local_sem.at[1])
    load_vel.start()
    load_scal.start()

    barrier = pltpu.get_barrier_semaphore()
    for axis in sizes:

        @pl.when(me[axis] > 0)
        def _():
            pl.semaphore_signal(
                barrier, inc=1, device_id={axis: me[axis] - 1}, device_id_type=MESH
            )

        @pl.when(me[axis] < ends[axis])
        def _():
            pl.semaphore_signal(
                barrier, inc=1, device_id={axis: me[axis] + 1}, device_id_type=MESH
            )

    for number, axis, up, land0, down, land1 in transfers:
        blank(axis, land0, land1)
    yb[:, 8:16] = jnp.zeros((NF, 8, CK), F32)
    yb[:, 24:128] = jnp.zeros((NF, 104, CK), F32)
    dz_in[16:128] = jnp.zeros((112, COLS), F32)
    xy_out[...] = jnp.zeros(xy_out.shape, F32)

    peers = 0
    for axis in sizes:
        peers = peers + jnp.minimum(me[axis], 1) + jnp.minimum(ends[axis] - me[axis], 1)
    pl.semaphore_wait(barrier, peers)

    send(*x_vel)
    send(*x_scal)
    load_vel.wait()
    load_scal.wait()

    for f in range(NF):
        for i in range(CI):
            y_out[0, f, i : i + 1, :] = fields[f, i, 0:1, :]
            y_out[1, f, i : i + 1, :] = fields[f, i, CJ - 1 : CJ, :]
    send(*y_rows)

    z_out[...] = jnp.zeros(z_out.shape, F32)
    for f in range(NF):
        for b in range(OWN // 128):
            block = fields[f, 2 * b : 2 * b + 2].reshape(128, CK).T
            z_out[0, f : f + 1, b * 128 : b * 128 + 128] = block[0:1]
            z_out[1, f : f + 1, b * 128 : b * 128 + 128] = block[CK - 1 : CK]
            hi, lo = split(block)
            a_hi[f * CK : f * CK + CK, b * 128 : b * 128 + 128] = hi
            a_lo[f * CK : f * CK + CK, b * 128 : b * 128 + 128] = lo

    arrive(*y_rows)
    for f in range(NF):
        block = yb[f].T
        z_out[0, f : f + 1, YB:COLS] = block[0:1]
        z_out[1, f : f + 1, YB:COLS] = block[CK - 1 : CK]
    send(*z_cols)
    for side, i in ((0, 0), (1, CI - 1)):
        for part in range(2):
            for f in range(NF):
                row = yb[f, 16 * part + i : 16 * part + i + 1, :]
                xy_out[side, 8 * part + f : 8 * part + f + 1, :] = row
    send(*xy_rows)

    where_i = li[...].reshape(1, n).astype(F32)
    where_j = lj[...].reshape(1, n).astype(F32)
    where_k = lk[...].reshape(1, n).astype(F32)
    row16 = iota((16, n), 0)
    plane = jnp.where(row16 == 8, -1, jnp.where(row16 == 9, CI, row16)).astype(F32)
    spread = tent(pos[0:1, :] - (plane - where_i))
    wi[...] = jnp.where(row16 < 10, spread, 0.0)
    wj = tent(pos[1:2, :] - (iota((CJ, n), 0).astype(F32) - where_j))
    wj_ends = (tent(pos[1:2, :] - (-1.0 - where_j)), tent(pos[1:2, :] - (float(CJ) - where_j)))
    lines[...] = tent(pos[2:3, :] - (iota((CK, n), 0).astype(F32) - where_k))
    line_ends[0:1, :] = tent(pos[2:3, :] - (-1.0 - where_k))
    line_ends[1:2, :] = tent(pos[2:3, :] - (float(CK) - where_k))
    for i in range(10):
        hi, lo = split(wi[i : i + 1, :] * wj)
        s_hi[i * CJ : i * CJ + CJ, :] = hi
        s_lo[i * CJ : i * CJ + CJ, :] = lo
    for part in range(2):
        hi, lo = split(wi[...] * wj_ends[part])
        s_hi[YB + 16 * part : YB + 16 * part + 16, :] = hi
        s_lo[YB + 16 * part : YB + 16 * part + 16, :] = lo
    s_hi[YB + 32 : COLS, :] = jnp.zeros((96, n), BF16)
    s_lo[YB + 32 : COLS, :] = jnp.zeros((96, n), BF16)

    arrive(*z_cols)
    for part in range(2):
        xz_out[0, 8 * part : 8 * part + 8, 0:128] = z_in[8 * part : 8 * part + 8, 0:128]
        xz_out[1, 8 * part : 8 * part + 8, 0:128] = z_in[8 * part : 8 * part + 8, OWN - 128 : OWN]
        for side in range(2):
            xz_out[side, 8 * part : 8 * part + 8, 128:256] = z_in[8 * part : 8 * part + 8, YB:COLS]
    send(*xz_cols)
    hi, lo = split(z_in[:, 0:OWN])
    a_hi[NF * CK : ROWS, 0:OWN] = hi
    a_lo[NF * CK : ROWS, 0:OWN] = lo

    def pick(columns, chunk):
        left = jnp.concatenate([a_hi[:, columns], a_hi[:, columns], a_lo[:, columns]], axis=1)
        right = jnp.concatenate(
            [s_hi[columns, chunk], s_lo[columns, chunk], s_hi[columns, chunk]], axis=0
        )
        return jnp.dot(left, right, preferred_element_type=F32)

    chunks = [slice(c * 256, c * 256 + 256) for c in range(n // 256)]
    for chunk in chunks:
        picked[:, chunk] = pick(slice(0, OWN), chunk)

    arrive(*xy_rows)
    for part in range(2):
        for f in range(NF):
            for side in range(2):
                row = xy_in[side, 8 * part + f : 8 * part + f + 1, :]
                yb[f, 16 * part + 8 + side : 16 * part + 9 + side, :] = row
    arrive(*xz_cols)
    lane = iota((16, 128), 1)
    x_part = jnp.where(
        lane < CJ,
        pltpu.roll(xz_in[0, :, 0:128], 64, 1),
        pltpu.roll(xz_in[1, :, 0:128], 64, 1),
    )
    lane16 = lane % 16
    y_part = jnp.where(
        lane16 == 8,
        pltpu.roll(xz_in[0, :, 128:256], 1, 1),
        jnp.where(lane16 == 9, pltpu.roll(xz_in[1, :, 128:256], 9, 1), z_in[:, YB:COLS]),
    )
    for column, part in ((XB, x_part), (YB, y_part)):
        hi, lo = split(part)
        a_hi[NF * CK : ROWS, column : column + 128] = hi
        a_lo[NF * CK : ROWS, column : column + 128] = lo
    for f in range(NF):
        hi, lo = split(yb[f].T)
        a_hi[f * CK : f * CK + CK, YB:COLS] = hi
        a_lo[f * CK : f * CK + CK, YB:COLS] = lo
    arrive(*x_vel)
    arrive(*x_scal)
    for f in range(NF):
        hi, lo = split(xb[f].T)
        a_hi[f * CK : f * CK + CK, XB:YB] = hi
        a_lo[f * CK : f * CK + CK, XB:YB] = lo

    for chunk in chunks:
        value = picked[:, chunk] + pick(slice(OWN, COLS), chunk)
        for f in range(NF):
            total = jnp.sum(value[f * CK : f * CK + CK] * lines[:, chunk], axis=0, keepdims=True)
            for part in range(2):
                row = NF * CK + 8 * part + f
                total = total + value[row : row + 1] * line_ends[part : part + 1, chunk]
            gathered[f : f + 1, chunk] = total

    motion = mot[...]
    warmth = heat[...].reshape(1, n)
    q = diam[...].reshape(1, n)
    gas = gathered[0:3, :]
    gas_heat, moisture, rho = gathered[3:4, :], gathered[4:5, :], gathered[5:6, :]
    drag = step_time / (0.5 * q)
    new_motion = (motion + drag * gas) / (1.0 + drag)
    mass = q * jnp.sqrt(q)
    vapour = jnp.exp(4.0 * (warmth - 1.0))
    decay = step_time * evap_rate * rho * (vapour - moisture)
    new_q = q - decay
    new_mass = new_q * jnp.sqrt(new_q)
    conduction = step_time * heat_rate * rho / q
    new_heat = (warmth + conduction * gas_heat) / (1.0 + conduction) - (
        boiling_energy_drain * decay / q
    )
    live = iota((1, n), 1) // TILE < tally[0]
    state[0:3, :] = jnp.where(live, new_motion, motion)
    state[3:4, :] = jnp.where(live, new_heat, warmth)
    state[4:5, :] = jnp.where(live, new_q, q)
    mass = jnp.where(live, mass, 0.0)
    terms = [mass * (motion[c : c + 1] - new_motion[c : c + 1]) for c in range(3)]
    terms.append(mass * (warmth - new_heat))
    terms.append(jnp.where(live, mass - new_mass, 0.0))

    for c in range(NS):
        hi, lo = split(terms[c] * lines[...])
        t_hi[c * CK : c * CK + CK, :] = hi
        t_lo[c * CK : c * CK + CK, :] = lo
    packed = jnp.concatenate(terms + [jnp.zeros((3, n), F32)], axis=0)
    tail = jnp.concatenate([packed * line_ends[0:1, :], packed * line_ends[1:2, :]], axis=0)
    hi, lo = split(tail)
    t_hi[NS * CK : NS * CK + 16, :] = hi
    t_lo[NS * CK : NS * CK + 16, :] = lo
    t_hi[NS * CK + 16 : COLS, :] = jnp.zeros((112, n), BF16)
    t_lo[NS * CK + 16 : COLS, :] = jnp.zeros((112, n), BF16)

    def spill(line, column):
        left = jnp.concatenate([s_hi[line, :], s_lo[line, :], s_hi[line, :]], axis=1)
        right = jnp.concatenate([t_hi[column, :], t_hi[column, :], t_lo[column, :]], axis=1)
        return lax.dot_general(
            left, right, (((1,), (1,)), ((), ())), preferred_element_type=F32
        )

    def put_z(block, column):
        dz_out[:, column : column + 128] = block.T[0:16]

    rim = slice(OWN, COLS)
    for w in range(3):
        value = spill(rim, slice(w * 256, w * 256 + 256))
        for h in range(2):
            c = 2 * w + h
            half = value[:, h * 128 : h * 128 + 128]
            if c < NS:
                dx_out[0, :, c * CK : c * CK + CK] = half[0:64]
                dx_out[1, :, c * CK : c * CK + CK] = half[64:128]
                dy[:, c * CK : c * CK + CK] = half[128:160]
            else:
                put_z(half[0:128], XB)
                put_z(half[128:256], YB)
    send(*d_x)

    for w in (2, 0, 1):
        value = spill(slice(0, OWN), slice(w * 256, w * 256 + 256))
        for h in range(2):
            c = 2 * w + h
            half = value[:, h * 128 : h * 128 + 128]
            if c < NS:
                out[c] = half.reshape(CI, CJ, CK)
            else:
                for b in range(OWN // 128):
                    put_z(half[b * 128 : b * 128 + 128], b * 128)
        if w == 2:
            send(*d_z)

    lane128 = iota((128, 128), 1)

    def ends_of(columns, c):
        return jnp.where(
            lane128 == 0,
            columns[:, c : c + 1],
            jnp.where(lane128 == CK - 1, columns[:, 8 + c : 9 + c], 0.0),
        )

    arrive(*d_z)
    y_cols = dz_in[:, YB:COLS].T
    for c in range(NS):
        at = slice(c * CK, c * CK + CK)
        dy[:, at] = dy[:, at] + ends_of(y_cols, c)[0:32]
    send(*d_y)
    for b in range(OWN // 128):
        columns = dz_in[:, b * 128 : b * 128 + 128].T
        for c in range(NS):
            add = ends_of(columns, c).reshape(2, CJ, CK)
            out[c, 2 * b : 2 * b + 2] = out[c, 2 * b : 2 * b + 2] + add

    arrive(*d_y)
    for side in range(2):
        dxe_out[side, 0:16, :] = dz_in[0:16, XB:YB]
        dxe_out[side, 16:32, :] = jnp.zeros((16, CK), F32)
        for part in range(2):
            for c in range(NS):
                row = dy_in[part, 8 + side : 9 + side, c * CK : c * CK + CK]
                dxe_out[side, 16 + 8 * part + c : 17 + 8 * part + c, :] = row
    send(*d_xe)
    for part in range(2):
        j = 0 if part == 0 else CJ - 1
        for c in range(NS):
            for i in range(CI):
                out[c, i, j : j + 1, :] = (
                    out[c, i, j : j + 1, :] + dy_in[part, i : i + 1, c * CK : c * CK + CK]
                )

    arrive(*d_xe)
    for side in range(2):
        i = 0 if side == 0 else CI - 1
        for part in range(2):
            j = 0 if part == 0 else CJ - 1
            for c in range(NS):
                row = 16 + 8 * part + c
                out[c, i, j : j + 1, :] = out[c, i, j : j + 1, :] + dxe_in[side, row : row + 1, :]
    x_cols = jnp.where(
        lane < CJ,
        pltpu.roll(dxe_in[0, 0:16, :], 64, 1),
        pltpu.roll(dxe_in[1, 0:16, :], 64, 1),
    )
    x_cols = jnp.concatenate([x_cols, jnp.zeros((112, 128), F32)], axis=0).T
    for c in range(NS):
        add = ends_of(x_cols, c)
        out[c, 0] = out[c, 0] + add[0:CJ]
        out[c, CI - 1] = out[c, CI - 1] + add[CJ:128]

    arrive(*d_x)
    for side in range(2):
        i = 0 if side == 0 else CI - 1
        for c in range(NS):
            out[c, i] = out[c, i] + dx_in[side, :, c * CK : c * CK + CK]

    for transfer in transfers:
        sent(*transfer)


def local(sizes, vel, scal, pos, mot, heat, diam, li, lj, lk, tally):
    n = heat.shape[0]
    vmem = pl.BlockSpec(memory_space=pltpu.VMEM)
    hbm = pl.BlockSpec(memory_space=pl.ANY)
    return pl.pallas_call(
        functools.partial(kernel, sizes),
        out_shape=(
            jax.ShapeDtypeStruct((NS, CI, CJ, CK), F32),
            jax.ShapeDtypeStruct((NS, n), F32),
        ),
        in_specs=[hbm, hbm] + [vmem] * 7 + [pl.BlockSpec(memory_space=pltpu.SMEM)],
        out_specs=(vmem, vmem),
        scratch_shapes=[
            pltpu.VMEM((NF, CI, CJ, CK), F32),
            pltpu.VMEM((ROWS, COLS), BF16),
            pltpu.VMEM((ROWS, COLS), BF16),
            pltpu.VMEM((COLS, n), BF16),
            pltpu.VMEM((COLS, n), BF16),
            pltpu.VMEM((COLS, n), BF16),
            pltpu.VMEM((COLS, n), BF16),
            pltpu.VMEM((ROWS, n), F32),
            pltpu.VMEM((16, n), F32),
            pltpu.VMEM((CK, n), F32),
            pltpu.VMEM((8, n), F32),
            pltpu.VMEM((8, n), F32),
            pltpu.VMEM((NF, 128, CK), F32),
            pltpu.VMEM((NF, 128, CK), F32),
            pltpu.VMEM((2, NF, 8, CK), F32),
            pltpu.VMEM((2, 8, COLS), F32),
            pltpu.VMEM((16, COLS), F32),
            pltpu.VMEM((2, 16, 256), F32),
            pltpu.VMEM((2, 16, 256), F32),
            pltpu.VMEM((2, 16, CK), F32),
            pltpu.VMEM((2, 16, CK), F32),
            pltpu.VMEM((2, CJ, NS * CK), F32),
            pltpu.VMEM((2, CJ, NS * CK), F32),
            pltpu.VMEM((32, NS * CK), F32),
            pltpu.VMEM((2, 16, NS * CK), F32),
            pltpu.VMEM((16, COLS), F32),
            pltpu.VMEM((128, COLS), F32),
            pltpu.VMEM((2, 32, CK), F32),
            pltpu.VMEM((2, 32, CK), F32),
            pltpu.SemaphoreType.DMA((2,)),
            pltpu.SemaphoreType.DMA((20,)),
            pltpu.SemaphoreType.DMA((20,)),
        ],
        compiler_params=pltpu.CompilerParams(
            collective_id=0, has_side_effects=True, vmem_limit_bytes=60 * 1024 * 1024
        ),
    )(vel, scal, pos, mot, heat, diam, li, lj, lk, tally)


def solution(mesh):
    sizes = {axis: mesh.shape[axis] for axis in ("gx", "gy", "gz")}
    flat = P(("gx", "gy", "gz"))
    wide = P(None, ("gx", "gy", "gz"))
    grid = P(None, "gx", "gy", "gz")
    return jax.shard_map(
        functools.partial(local, sizes),
        mesh=mesh,
        in_specs=(grid, grid, wide, wide) + (flat,) * 6,
        out_specs=(grid, wide),
        check_vma=False,
    )
```

profile of v0, /device:TPU:71, one launch (start us, length us, event | category | flops | bytes accessed | tf_op | source)
XLA Modules:
  0.0 45.2 jit_solution(2951536951614198325)
XLA Ops:
  1.3 40.8 %shard_map.113 = (f32[5,8,64,128]{3,2,1,0:T(8,128)}, f32[5,1024]{1,0:T(8,128)}) custom-call(f32[3,8,64,128]{3,2,1,0:T(8,128)} %vel.1, f32[3,8,64,128]{3,2,1,0:T(8,128)} %scal.1, f32[3,1024]{1,0:T(4,128)} %pos.1, f32[3,1024]{1,0:T(4,128)} %mot.1, f32[1024]{0:T(1024)} %heat.1, f32[1024]{0:T(1024)} %diam.1, s32[1024]{0:T(1024)} %li.1, s32[1024]{0:T(1024)} %lj.1, ...), custom_call_target="tpu_custom_call" | custom-call | tf_op jit(solution)/shard_map/pallas_call | solution.py:451
  42.1 0.0 copy-start
  42.1 2.5 %copy.15 = f32[5,8,64,128]{3,2,1,0:T(8,128)} copy(f32[5,8,64,128]{3,2,1,0:T(8,128)} %get-tuple-element.4) | data formatting | bytes 2621440
  44.6 0.0 copy-done
  44.6 0.6 %copy.16 = f32[5,1024]{1,0:T(8,128)} copy(f32[5,1024]{1,0:T(8,128)S(1)} %copy-done) | data formatting | bytes 40960
Async XLA Ops:
  42.1 2.5 %copy-start = (f32[5,1024]{1,0:T(8,128)S(1)}, f32[5,1024]{1,0:T(8,128)}, u32[]{:S(2)}) copy-start(f32[5,1024]{1,0:T(8,128)} %get-tuple-element.5) | copy-start | bytes 61444
where the time goes:
time: 45.4 us; the launch traced here: 45.2 us
  Pallas kernels  40.8 us (90%)
  local copies, waits for them, and re-layouts  3.15 us (7%)
  between operations  1.3 us (3%)
    pallas_call x1, Pallas kernels, local(): pl.pallas_call(functools.partial(kernel, sizes), out_shape=(jax.ShapeDtyp...  40.8 us
    unnamed x4, local copies, waits for them, and re-layouts  3.15 us

commit v1 on v0

v1 whole, which is shorter than its diff:
```python
import functools

import jax
import jax.numpy as jnp
from jax import lax
from jax.experimental import pallas as pl
from jax.experimental.pallas import tpu as pltpu
from jax.sharding import PartitionSpec as P

TILE = 128
NF = 6
NS = 5
CI, CJ, CK = 8, 64, 128
OWN = CI * CJ
COLS = OWN + 128
ROWS = NF * CK + 16
MESH = pl.DeviceIdType.MESH
F32 = jnp.float32
BF16 = jnp.bfloat16

step_time = 0.25
evap_rate = 1.0
heat_rate = 2.0
boiling_energy_drain = 0.3


def split(x):
    hi = x.astype(BF16)
    return hi, (x - hi.astype(F32)).astype(BF16)


def tent(offset):
    return jnp.maximum(0.0, 1.0 - jnp.abs(offset))


def iota(shape, dim):
    return lax.broadcasted_iota(jnp.int32, shape, dim)


def kernel(
    sizes,
    vel,
    scal,
    pos_hbm,
    mot_hbm,
    heat_hbm,
    diam_hbm,
    li_hbm,
    lj_hbm,
    lk_hbm,
    tally,
    out,
    state,
    fields,
    pos,
    mot,
    heat,
    diam,
    li,
    lj,
    lk,
    mine,
    theirs,
    a_hi,
    a_lo,
    s_hi,
    s_lo,
    t_hi,
    t_lo,
    e_lhs,
    l_hi,
    l_lo,
    u_hi,
    u_lo,
    ws,
    ws_ends,
    wi,
    lines,
    line_ends,
    gathered,
    part_out,
    part_in,
    terms_out,
    terms_in,
    yb,
    y_out,
    z_out,
    z_in,
    yz_in,
    dy,
    dy_in,
    dz_out,
    dz_in,
    dyz_in,
    local_sem,
    send_sem,
    recv_sem,
):
    n = pos.shape[1]
    axes = tuple(sizes)
    me = {axis: lax.axis_index(axis) for axis in axes}
    ends = {axis: size - 1 for axis, size in sizes.items()}

    def there(steps):
        found = None
        for axis, step in steps:
            one = me[axis] < ends[axis] if step > 0 else me[axis] > 0
            found = one if found is None else jnp.logical_and(found, one)
        return found

    def peer(steps):
        return {axis: me[axis] + step for axis, step in steps}

    def back(steps):
        return tuple((axis, -step) for axis, step in steps)

    numbers = iter(range(64))

    def both(axis, up, land0, down, land1):
        return (
            (next(numbers), ((axis, 1),), up, land0),
            (next(numbers), ((axis, -1),), down, land1),
        )

    def corners(source, land):
        found = []
        for y in (1, -1):
            for z in (1, -1):
                sides = (0 if y > 0 else 1, 0 if z > 0 else 1)
                steps = (("gy", y), ("gz", z))
                found.append((next(numbers), steps, source(1 - sides[1]), land.at[sides]))
        return tuple(found)

    def copy(transfer, steps):
        number, _, source, land = transfer
        return pltpu.make_async_remote_copy(
            src_ref=source,
            dst_ref=land,
            send_sem=send_sem.at[number],
            recv_sem=recv_sem.at[number],
            device_id=peer(steps),
            device_id_type=MESH,
        )

    def send(group):
        for transfer in group:
            pl.when(there(transfer[1]))(lambda t=transfer: copy(t, t[1]).start())

    def arrive(group):
        for transfer in group:
            steps = back(transfer[1])
            pl.when(there(steps))(lambda t=transfer, s=steps: copy(t, s).wait_recv())

    def sent(group):
        for transfer in group:
            pl.when(there(transfer[1]))(lambda t=transfer: copy(t, t[1]).wait_send())

    def blank(group):
        for _, steps, _, land in group:

            @pl.when(jnp.logical_not(there(back(steps))))
            def _():
                land[...] = jnp.zeros(land.shape, F32)

    g_pos = both("gx", mine, theirs.at[0], mine, theirs.at[1])
    g_y = both("gy", y_out.at[1], yb.at[:, 0:8], y_out.at[0], yb.at[:, 16:24])
    g_z = both("gz", z_out.at[1], z_in.at[0:8], z_out.at[0], z_in.at[8:16])
    g_yz = corners(lambda side: z_out.at[side], yz_in)
    g_part = both("gx", part_out.at[1], part_in.at[0], part_out.at[0], part_in.at[1])
    d_terms = both("gx", terms_out, terms_in.at[0], terms_out, terms_in.at[1])
    d_z = both(
        "gz",
        dz_out.at[8:16, 0:OWN],
        dz_in.at[0:8],
        dz_out.at[0:8, 0:OWN],
        dz_in.at[8:16],
    )
    d_y = both("gy", dy.at[16:24], dy_in.at[0], dy.at[0:8], dy_in.at[1])
    d_yz = corners(lambda side: dz_out.at[8 * side : 8 * side + 8, OWN:COLS], dyz_in)
    groups = (g_pos, g_y, g_z, g_yz, g_part, d_terms, d_z, d_y, d_yz)

    loads = []
    for number, (source, land) in enumerate(
        (
            (pos_hbm, pos),
            (li_hbm, li),
            (lj_hbm, lj),
            (lk_hbm, lk),
            (vel, fields.at[0:3]),
            (scal, fields.at[3:6]),
            (mot_hbm, mot),
            (heat_hbm, heat),
            (diam_hbm, diam),
        )
    ):
        loads.append(pltpu.make_async_copy(source, land, local_sem.at[number]))
        loads[-1].start()

    barrier = pltpu.get_barrier_semaphore()
    for _, steps, _, _ in g_pos + g_y + g_z + g_yz:
        pl.when(there(steps))(
            lambda s=steps: pl.semaphore_signal(
                barrier, inc=1, device_id=peer(s), device_id_type=MESH
            )
        )

    for group in groups:
        blank(group)
    yb[:, 8:16] = jnp.zeros((NF, 8, CK), F32)
    yb[:, 24:128] = jnp.zeros((NF, 104, CK), F32)
    z_out[...] = jnp.zeros(z_out.shape, F32)
    part_out[:, 6:8] = jnp.zeros((2, 2, n), F32)
    for x in range(2):
        l_hi[x, CK : 2 * CK] = jnp.zeros((CK, n), BF16)
        l_lo[x, CK : 2 * CK] = jnp.zeros((CK, n), BF16)
    s_hi[OWN + 32 : COLS] = jnp.zeros((96, n), BF16)
    s_lo[OWN + 32 : COLS] = jnp.zeros((96, n), BF16)
    t_hi[NS * CK + 16 :] = jnp.zeros((112, n), BF16)
    t_lo[NS * CK + 16 :] = jnp.zeros((112, n), BF16)

    for load in loads[0:4]:
        load.wait()
    mine[0:3] = pos[...]
    for axis, cell in enumerate((li, lj, lk)):
        mine[3 + axis : 4 + axis] = cell[...].reshape(1, n).astype(F32)
    mine[6:8] = jnp.zeros((2, n), F32)

    near = {axis: jnp.minimum(me[axis], 1) + jnp.minimum(ends[axis] - me[axis], 1) for axis in axes}
    pl.semaphore_wait(barrier, near["gx"] + near["gy"] + near["gz"] + near["gy"] * near["gz"])
    send(g_pos)

    for load in loads[4:]:
        load.wait()
    for f in range(NF):
        for i in range(CI):
            y_out[0, f, i : i + 1, :] = fields[f, i, 0:1, :]
            y_out[1, f, i : i + 1, :] = fields[f, i, CJ - 1 : CJ, :]
    send(g_y)

    for f in range(NF):
        for b in range(OWN // 128):
            block = fields[f, 2 * b : 2 * b + 2].reshape(128, CK).T
            z_out[0, f : f + 1, b * 128 : b * 128 + 128] = block[0:1]
            z_out[1, f : f + 1, b * 128 : b * 128 + 128] = block[CK - 1 : CK]
            hi, lo = split(block)
            a_hi[f * CK : f * CK + CK, b * 128 : b * 128 + 128] = hi
            a_lo[f * CK : f * CK + CK, b * 128 : b * 128 + 128] = lo
    send(g_z)
    send(g_yz)

    def ramp(rows):
        return iota((rows, n), 0).astype(F32)

    row16 = iota((16, n), 0)
    spread = tent(mine[0:1] - (ramp(16) - mine[3:4]))
    wi[...] = jnp.where(row16 < CI, spread, 0.0)
    wj = tent(mine[1:2] - (ramp(CJ) - mine[4:5]))
    wj_ends = (tent(mine[1:2] - (-1.0 - mine[4:5])), tent(mine[1:2] - (float(CJ) - mine[4:5])))
    lines[...] = tent(mine[2:3] - (ramp(CK) - mine[5:6]))
    line_ends[0:1] = tent(mine[2:3] - (-1.0 - mine[5:6]))
    line_ends[1:2] = tent(mine[2:3] - (float(CK) - mine[5:6]))
    for i in range(CI):
        hi, lo = split(wi[i : i + 1] * wj)
        s_hi[i * CJ : i * CJ + CJ] = hi
        s_lo[i * CJ : i * CJ + CJ] = lo
    for y in range(2):
        hi, lo = split(wi[...] * wj_ends[y])
        s_hi[OWN + 16 * y : OWN + 16 * y + 16] = hi
        s_lo[OWN + 16 * y : OWN + 16 * y + 16] = lo

    lane16 = iota((16, 128), 1)
    arrive(g_y)
    for f in range(NF):
        hi, lo = split(yb[f].T)
        a_hi[f * CK : f * CK + CK, OWN:COLS] = hi
        a_lo[f * CK : f * CK + CK, OWN:COLS] = lo
    arrive(g_z)
    hi, lo = split(z_in[...])
    a_hi[NF * CK : ROWS, 0:OWN] = hi
    a_lo[NF * CK : ROWS, 0:OWN] = lo
    arrive(g_yz)
    corner = jnp.zeros((16, 128), F32)
    for y in range(2):
        for i in range(CI):
            at = i * CJ + (CJ - 1 if y == 0 else 0)
            first = at // 128 * 128
            block = jnp.concatenate([yz_in[y, z, :, first : first + 128] for z in range(2)], axis=0)
            to = 16 * y + i
            moved = pltpu.roll(block, (to - at) % 128, 1)
            corner = jnp.where(lane16 == to, moved, corner)
    hi, lo = split(corner)
    a_hi[NF * CK : ROWS, OWN:COLS] = hi
    a_lo[NF * CK : ROWS, OWN:COLS] = lo

    def z_block(value):
        hi, lo = split(value)
        hi, lo = hi.astype(F32), lo.astype(F32)
        return (hi + pltpu.roll(hi, 16, 1) + pltpu.roll(lo, 32, 1)).astype(BF16)

    def put_plane(x, at, rows, value, ends_value):
        hi, lo = split(value)
        e_lhs[x, at : at + rows, 0:128] = hi
        e_lhs[x, at : at + rows, 128:256] = hi
        e_lhs[x, at : at + rows, 256:384] = lo
        e_lhs[x, at : at + rows, 384:512] = z_block(ends_value)

    lane64 = iota((CJ, 128), 1)
    lane8 = iota((8, 128), 1)
    for x in range(2):
        i = 0 if x == 0 else CI - 1
        first = i * CJ // 128 * 128
        columns = jnp.concatenate(
            [z_in[:, first : first + 128], jnp.zeros((112, 128), F32)], axis=0
        ).T
        columns = columns[0:CJ] if x == 0 else columns[CJ:128]
        for f in range(NF):
            moved = columns if f == 0 else pltpu.roll(columns, 128 - f, 1)
            moved = jnp.where((lane64 == 0) | (lane64 == 8), moved, 0.0)
            put_plane(x, f * CJ, CJ, fields[f, i], moved)
        values, moves = [], []
        for y in range(2):
            values += [yb[f, 16 * y + i : 16 * y + i + 1, :] for f in range(NF)]
            values.append(jnp.zeros((2, CK), F32))
            at = i * CJ + (CJ - 1 if y == 0 else 0)
            first = at // 128 * 128
            total = jnp.zeros((8, 128), F32)
            for z in range(2):
                block = pltpu.roll(yz_in[y, z, :, first : first + 128], (8 * z - at) % 128, 1)
                total = jnp.where(lane8 == 8 * z, block, total)
            moves.append(total)
        put_plane(
            x, NF * CJ, 16, jnp.concatenate(values, axis=0), jnp.concatenate(moves, axis=0)
        )

    chunks = [slice(c * 256, c * 256 + 256) for c in range(n // 256)]

    def gather(chunk):
        left = jnp.concatenate([a_hi[...], a_hi[...], a_lo[...]], axis=1)
        right = jnp.concatenate([s_hi[:, chunk], s_lo[:, chunk], s_hi[:, chunk]], axis=0)
        value = jnp.dot(left, right, preferred_element_type=F32)
        for f in range(NF):
            total = jnp.sum(value[f * CK : f * CK + CK] * lines[:, chunk], axis=0, keepdims=True)
            for z in range(2):
                row = NF * CK + 8 * z + f
                total = total + value[row : row + 1] * line_ends[z : z + 1, chunk]
            gathered[f : f + 1, chunk] = total

    for chunk in chunks[:2]:
        gather(chunk)

    arrive(g_pos)
    for x in range(2):
        p = theirs.at[x]
        reach = tent(p[0:1] - ((float(CI) if x == 0 else -1.0) - p[3:4]))
        ws[x] = reach * tent(p[1:2] - (ramp(CJ) - p[4:5]))
        ws_ends[x, 0:1] = reach * tent(p[1:2] - (-1.0 - p[4:5]))
        ws_ends[x, 1:2] = reach * tent(p[1:2] - (float(CJ) - p[4:5]))
        hi, lo = split(tent(p[2:3] - (ramp(CK) - p[5:6])))
        l_hi[x, 0:CK] = hi
        l_lo[x, 0:CK] = lo
        low = tent(p[2:3] - (-1.0 - p[5:6]))
        high = tent(p[2:3] - (float(CK) - p[5:6]))
        hi, lo = split(jnp.where(row16 == 0, low, jnp.where(row16 == 8, high, 0.0)))
        l_hi[x, CK : CK + 16] = hi
        l_lo[x, CK : CK + 16] = lo
    for x in range(2):
        for chunk in chunks:
            top, low = l_hi[x, 0:CK, chunk], l_lo[x, 0:CK, chunk]
            top_z, low_z = l_hi[x, CK : CK + 16, chunk], l_lo[x, CK : CK + 16, chunk]
            right = jnp.concatenate(
                [top, low, top, top_z, low_z, top_z, jnp.zeros((80, 256), BF16)], axis=0
            )
            value = jnp.dot(e_lhs[x], right, preferred_element_type=F32)
            last = NF * CJ
            total = value[last : last + 8] * ws_ends[x, 0:1, chunk]
            total = total + value[last + 8 : last + 16] * ws_ends[x, 1:2, chunk]
            weight = ws[x, :, chunk]
            for f in range(NF):
                row = jnp.sum(value[f * CJ : f * CJ + CJ] * weight, axis=0, keepdims=True)
                part_out[x, f : f + 1, chunk] = row + total[f : f + 1]
    send(g_part)

    for chunk in chunks[2:]:
        gather(chunk)

    motion = mot[...]
    warmth = heat[...].reshape(1, n)
    q = diam[...].reshape(1, n)
    live = iota((1, n), 1) // TILE < tally[0]
    arrive(g_part)
    got = gathered[0:NF] + part_in[0, 0:NF] + part_in[1, 0:NF]
    gas = got[0:3]
    gas_heat, moisture, rho = got[3:4], got[4:5], got[5:6]
    drag = step_time / (0.5 * q)
    new_motion = (motion + drag * gas) / (1.0 + drag)
    mass = q * jnp.sqrt(q)
    vapour = jnp.exp(4.0 * (warmth - 1.0))
    decay = step_time * evap_rate * rho * (vapour - moisture)
    new_q = q - decay
    new_mass = new_q * jnp.sqrt(new_q)
    conduction = step_time * heat_rate * rho / q
    new_heat = (warmth + conduction * gas_heat) / (1.0 + conduction) - (
        boiling_energy_drain * decay / q
    )
    state[0:3] = jnp.where(live, new_motion, motion)
    state[3:4] = jnp.where(live, new_heat, warmth)
    state[4:5] = jnp.where(live, new_q, q)
    terms_out[0:3] = jnp.where(live, mass * (motion - new_motion), 0.0)
    terms_out[3:4] = jnp.where(live, mass * (warmth - new_heat), 0.0)
    terms_out[4:5] = jnp.where(live, mass - new_mass, 0.0)
    terms_out[5:8] = jnp.zeros((3, n), F32)
    send(d_terms)

    for c in range(NS):
        hi, lo = split(terms_out[c : c + 1] * lines[...])
        t_hi[c * CK : c * CK + CK] = hi
        t_lo[c * CK : c * CK + CK] = lo
    tail = jnp.concatenate(
        [terms_out[...] * line_ends[0:1], terms_out[...] * line_ends[1:2]], axis=0
    )
    hi, lo = split(tail)
    t_hi[NS * CK : NS * CK + 16] = hi
    t_lo[NS * CK : NS * CK + 16] = lo

    def cross(left, right):
        return lax.dot_general(
            left, right, (((1,), (1,)), ((), ())), preferred_element_type=F32
        )

    lines_used = slice(0, OWN + 32)
    for w in range(3):
        column = slice(w * 256, w * 256 + 256)
        left = jnp.concatenate(
            [s_hi[lines_used], s_lo[lines_used], s_hi[lines_used]], axis=1
        )
        right = jnp.concatenate([t_hi[column], t_hi[column], t_lo[column]], axis=1)
        value = cross(left, right)
        for h in range(2):
            c = 2 * w + h
            half = value[:, h * 128 : h * 128 + 128]
            if c < NS:
                out[c] = half[0:OWN].reshape(CI, CJ, CK)
                dy[:, c * CK : c * CK + CK] = half[OWN : OWN + 32]
            else:
                for b in range(OWN // 128):
                    dz_out[:, b * 128 : b * 128 + 128] = half[b * 128 : b * 128 + 128].T[0:16]
                rest = jnp.concatenate([half[OWN : OWN + 32], jnp.zeros((96, 128), F32)], axis=0)
                dz_out[:, OWN:COLS] = rest.T[0:16]

    arrive(d_terms)
    lane1 = iota((1, 128), 1)
    for x in range(2):
        i = 0 if x == 0 else CI - 1
        weight = ws[x]
        for c in range(NS):
            hi, lo = split(terms_in[x, c : c + 1] * weight)
            u_hi[c * CJ : c * CJ + CJ] = hi
            u_lo[c * CJ : c * CJ + CJ] = lo
        last = NS * CJ
        for y in range(2):
            hi, lo = split(
                jnp.concatenate(
                    [terms_in[x] * ws_ends[x, y : y + 1], jnp.zeros((8, n), F32)], axis=0
                )
            )
            u_hi[last + 16 * y : last + 16 * y + 16] = hi
            u_lo[last + 16 * y : last + 16 * y + 16] = lo
        left = jnp.concatenate([u_hi[...], u_hi[...], u_lo[...]], axis=1)
        right = jnp.concatenate([l_hi[x], l_lo[x], l_hi[x]], axis=1)
        value = cross(left, right)
        for c in range(NS):
            out[c, i] = out[c, i] + value[c * CJ : c * CJ + CJ, 0:CK]
            for y in range(2):
                row = 16 * y + i
                at = slice(c * CK, c * CK + CK)
                line = last + 16 * y + c
                dy[row : row + 1, at] = dy[row : row + 1, at] + value[line : line + 1, 0:CK]
        first = i * CJ // 128 * 128
        keep = lane1 < CJ if x == 0 else lane1 >= CJ
        for b in range(3):
            block = value[b * 128 : min(b * 128 + 128, last + 32), CK : 2 * CK]
            if b == 2:
                block = jnp.concatenate([block, jnp.zeros((32, 128), F32)], axis=0)
            block = block.T
            for c in range(2 * b, min(2 * b + 2, NS)):
                for z in range(2):
                    row = block[8 * z : 8 * z + 1]
                    if c % 2 != x:
                        row = pltpu.roll(row, CJ, 1)
                    at = 8 * z + c
                    old = dz_out[at : at + 1, first : first + 128]
                    dz_out[at : at + 1, first : first + 128] = old + jnp.where(keep, row, 0.0)
        for y in range(2):
            block = value[last + 16 * y : last + 16 * y + 8, CK : 2 * CK]
            to = 16 * y + i
            for z in range(2):
                moved = pltpu.roll(block, (to - 8 * z) % 128, 1)
                old = dz_out[8 * z : 8 * z + 8, OWN:COLS]
                dz_out[8 * z : 8 * z + 8, OWN:COLS] = old + jnp.where(lane8 == to, moved, 0.0)
    send(d_z)
    send(d_yz)
    send(d_y)

    arrive(d_yz)
    arrive(d_z)
    lane128 = iota((128, 128), 1)
    for b in range(OWN // 128):
        block = dz_in[:, b * 128 : b * 128 + 128]
        for i in (2 * b, 2 * b + 1):
            for y in range(2):
                to = i * CJ % 128 + (0 if y == 0 else CJ - 1)
                at = (16 if y == 0 else 0) + i
                moved = jnp.concatenate([dyz_in[y, 0], dyz_in[y, 1]], axis=0)
                moved = pltpu.roll(moved, (to - at) % 128, 1)
                block = block + jnp.where(lane16 == to, moved, 0.0)
        columns = jnp.concatenate([block, jnp.zeros((112, 128), F32)], axis=0).T
        for c in range(NS):
            add = jnp.where(
                lane128 == 0,
                columns[:, c : c + 1],
                jnp.where(lane128 == CK - 1, columns[:, 8 + c : 9 + c], 0.0),
            ).reshape(2, CJ, CK)
            out[c, 2 * b : 2 * b + 2] = out[c, 2 * b : 2 * b + 2] + add
    arrive(d_y)
    for y in range(2):
        j = 0 if y == 0 else CJ - 1
        for c in range(NS):
            for i in range(CI):
                out[c, i, j : j + 1, :] = (
                    out[c, i, j : j + 1, :] + dy_in[y, i : i + 1, c * CK : c * CK + CK]
                )

    for group in groups:
        sent(group)


def local(sizes, vel, scal, pos, mot, heat, diam, li, lj, lk, tally):
    n = heat.shape[0]
    vmem = pl.BlockSpec(memory_space=pltpu.VMEM)
    hbm = pl.BlockSpec(memory_space=pltpu.HBM)
    planes = NF * CJ + 16
    return pl.pallas_call(
        functools.partial(kernel, sizes),
        out_shape=(
            jax.ShapeDtypeStruct((NS, CI, CJ, CK), F32),
            jax.ShapeDtypeStruct((NS, n), F32),
        ),
        in_specs=[hbm] * 9 + [pl.BlockSpec(memory_space=pltpu.SMEM)],
        out_specs=(vmem, vmem),
        scratch_shapes=[
            pltpu.VMEM((NF, CI, CJ, CK), F32),
            pltpu.VMEM((3, n), F32),
            pltpu.VMEM((3, n), F32),
            pltpu.VMEM((n,), F32),
            pltpu.VMEM((n,), F32),
            pltpu.VMEM((n,), jnp.int32),
            pltpu.VMEM((n,), jnp.int32),
            pltpu.VMEM((n,), jnp.int32),
            pltpu.VMEM((8, n), F32),
            pltpu.VMEM((2, 8, n), F32),
            pltpu.VMEM((ROWS, COLS), BF16),
            pltpu.VMEM((ROWS, COLS), BF16),
            pltpu.VMEM((COLS, n), BF16),
            pltpu.VMEM((COLS, n), BF16),
            pltpu.VMEM((768, n), BF16),
            pltpu.VMEM((768, n), BF16),
            pltpu.VMEM((2, planes, 512), BF16),
            pltpu.VMEM((2, 2 * CK, n), BF16),
            pltpu.VMEM((2, 2 * CK, n), BF16),
            pltpu.VMEM((NS * CJ + 32, n), BF16),
            pltpu.VMEM((NS * CJ + 32, n), BF16),
            pltpu.VMEM((2, CJ, n), F32),
            pltpu.VMEM((2, 8, n), F32),
            pltpu.VMEM((16, n), F32),
            pltpu.VMEM((CK, n), F32),
            pltpu.VMEM((8, n), F32),
            pltpu.VMEM((8, n), F32),
            pltpu.VMEM((2, 8, n), F32),
            pltpu.VMEM((2, 8, n), F32),
            pltpu.VMEM((8, n), F32),
            pltpu.VMEM((2, 8, n), F32),
            pltpu.VMEM((NF, 128, CK), F32),
            pltpu.VMEM((2, NF, 8, CK), F32),
            pltpu.VMEM((2, 8, OWN), F32),
            pltpu.VMEM((16, OWN), F32),
            pltpu.VMEM((2, 2, 8, OWN), F32),
            pltpu.VMEM((32, NS * CK), F32),
            pltpu.VMEM((2, 8, NS * CK), F32),
            pltpu.VMEM((16, COLS), F32),
            pltpu.VMEM((16, OWN), F32),
            pltpu.VMEM((2, 2, 8, 128), F32),
            pltpu.SemaphoreType.DMA((9,)),
            pltpu.SemaphoreType.DMA((22,)),
            pltpu.SemaphoreType.DMA((22,)),
        ],
        compiler_params=pltpu.CompilerParams(
            collective_id=0, has_side_effects=True, vmem_limit_bytes=32 * 1024 * 1024
        ),
    )(vel, scal, pos, mot, heat, diam, li, lj, lk, tally)


def solution(mesh):
    sizes = {axis: mesh.shape[axis] for axis in ("gx", "gy", "gz")}
    flat = P(("gx", "gy", "gz"))
    wide = P(None, ("gx", "gy", "gz"))
    grid = P(None, "gx", "gy", "gz")
    return jax.shard_map(
        functools.partial(local, sizes),
        mesh=mesh,
        in_specs=(grid, grid, wide, wide) + (flat,) * 6,
        out_specs=(grid, wide),
        check_vma=False,
    )
```

time: 45.4 us -> 41 us (0.903)
  Pallas kernels: 40.8 us -> 30.5 us
  local copies, waits for them, and re-layouts: 3.15 us -> 8.8 us
    pallas_call x1, Pallas kernels: 40.8 us -> 30.5 us  [local(): pl.pallas_call(functools.partial(kernel, sizes), out_shape=(jax.ShapeDtyp...]
    unnamed x4 -> x20, local copies, waits for them, and re-layouts: 3.15 us -> 8.8 us
where the time goes in v1:
time: 41 us; the launch traced here: 40.6 us
  Pallas kernels  30.5 us (74%)
  local copies, waits for them, and re-layouts  8.8 us (21%)
  between operations  1.31 us (3%)
    pallas_call x1, Pallas kernels, local(): pl.pallas_call(functools.partial(kernel, sizes), out_shape=(jax.ShapeDtyp...  30.5 us
    unnamed x20, local copies, waits for them, and re-layouts  8.8 us

profile of v1, /device:TPU:71, one launch (start us, length us, event | category | flops | bytes accessed | tf_op | source)
XLA Modules:
  0.0 40.6 jit_solution(15521230127112841750)
XLA Ops:
  1.3 0.0 copy-start
  1.3 1.1 %copy-done = f32[3,8,64,128]{3,2,1,0:T(8,128)S(1)} copy-done((f32[3,8,64,128]{3,2,1,0:T(8,128)S(1)}, f32[3,8,64,128]{3,2,1,0:T(8,128)}, u32[]{:S(2)}) %copy-start) | copy-done | bytes 786456
  2.4 0.0 copy-start.1
  2.4 1.1 %copy-done.1 = f32[3,8,64,128]{3,2,1,0:T(8,128)S(1)} copy-done((f32[3,8,64,128]{3,2,1,0:T(8,128)S(1)}, f32[3,8,64,128]{3,2,1,0:T(8,128)}, u32[]{:S(2)}) %copy-start.1) | copy-done | bytes 786456
  3.5 0.0 copy-start.2
  3.5 0.7 %copy-done.2 = f32[3,1024]{1,0:T(4,128)S(1)} copy-done((f32[3,1024]{1,0:T(4,128)S(1)}, f32[3,1024]{1,0:T(4,128)}, u32[]{:S(2)}) %copy-start.2) | copy-done | bytes 12312
  4.3 0.0 copy-start.3
  4.3 0.7 %copy-done.3 = f32[3,1024]{1,0:T(4,128)S(1)} copy-done((f32[3,1024]{1,0:T(4,128)S(1)}, f32[3,1024]{1,0:T(4,128)}, u32[]{:S(2)}) %copy-start.3) | copy-done | bytes 12312
  5.0 0.0 copy-start.4
  5.0 0.7 %copy-done.4 = f32[1024]{0:T(1024)S(1)} copy-done((f32[1024]{0:T(1024)S(1)}, f32[1024]{0:T(1024)}, u32[]{:S(2)}) %copy-start.4) | copy-done | bytes 4120
  5.7 0.0 copy-start.5
  5.7 0.7 %copy-done.5 = f32[1024]{0:T(1024)S(1)} copy-done((f32[1024]{0:T(1024)S(1)}, f32[1024]{0:T(1024)}, u32[]{:S(2)}) %copy-start.5) | copy-done | bytes 4120
  6.4 0.0 copy-start.6
  6.4 0.7 %copy-done.6 = s32[1024]{0:T(1024)S(1)} copy-done((s32[1024]{0:T(1024)S(1)}, s32[1024]{0:T(1024)}, u32[]{:S(2)}) %copy-start.6) | copy-done | bytes 4120
  7.0 0.0 copy-start.7
  7.0 0.7 %copy-done.7 = s32[1024]{0:T(1024)S(1)} copy-done((s32[1024]{0:T(1024)S(1)}, s32[1024]{0:T(1024)}, u32[]{:S(2)}) %copy-start.7) | copy-done | bytes 4120
  7.7 0.0 copy-start.8
  7.7 0.7 %copy-done.8 = s32[1024]{0:T(1024)S(1)} copy-done((s32[1024]{0:T(1024)S(1)}, s32[1024]{0:T(1024)}, u32[]{:S(2)}) %copy-start.8) | copy-done | bytes 4120
  8.4 30.5 %shard_map.113 = (f32[5,8,64,128]{3,2,1,0:T(8,128)S(1)}, f32[5,1024]{1,0:T(8,128)S(1)}) custom-call(f32[3,8,64,128]{3,2,1,0:T(8,128)S(1)} %copy-done, f32[3,8,64,128]{3,2,1,0:T(8,128)S(1)} %copy-done.1, f32[3,1024]{1,0:T(4,128)S(1)} %copy-done.2, f32[3,1024]{1,0:T(4,128)S(1)} %copy-done.3, f32[1024]{0:T(1024)S(1)} %copy-done.4, f32[1024]{0:T(1024)S(1)} %copy-done.5, ...), custom_call_target="tpu_custom_call" | custom-call | tf_op jit(solution)/shard_map/pallas_call | solution.py:542
  38.9 1.1 %copy.15 = f32[5,8,64,128]{3,2,1,0:T(8,128)} copy(f32[5,8,64,128]{3,2,1,0:T(8,128)S(1)} %get-tuple-element.4) | data formatting | bytes 2621440
  40.0 0.6 %copy.16 = f32[5,1024]{1,0:T(8,128)} copy(f32[5,1024]{1,0:T(8,128)S(1)} %get-tuple-element.5) | data formatting | bytes 40960
Async XLA Ops:
  1.3 1.1 %copy-start = (f32[3,8,64,128]{3,2,1,0:T(8,128)S(1)}, f32[3,8,64,128]{3,2,1,0:T(8,128)}, u32[]{:S(2)}) copy-start(f32[3,8,64,128]{3,2,1,0:T(8,128)} %vel.1) | copy-start | bytes 2359300
  2.4 1.1 %copy-start.1 = (f32[3,8,64,128]{3,2,1,0:T(8,128)S(1)}, f32[3,8,64,128]{3,2,1,0:T(8,128)}, u32[]{:S(2)}) copy-start(f32[3,8,64,128]{3,2,1,0:T(8,128)} %scal.1) | copy-start | bytes 2359300
  3.5 0.7 %copy-start.2 = (f32[3,1024]{1,0:T(4,128)S(1)}, f32[3,1024]{1,0:T(4,128)}, u32[]{:S(2)}) copy-start(f32[3,1024]{1,0:T(4,128)} %pos_hbm.1) | copy-start | bytes 36868
  4.3 0.7 %copy-start.3 = (f32[3,1024]{1,0:T(4,128)S(1)}, f32[3,1024]{1,0:T(4,128)}, u32[]{:S(2)}) copy-start(f32[3,1024]{1,0:T(4,128)} %mot_hbm.1) | copy-start | bytes 36868
  5.0 0.7 %copy-start.4 = (f32[1024]{0:T(1024)S(1)}, f32[1024]{0:T(1024)}, u32[]{:S(2)}) copy-start(f32[1024]{0:T(1024)} %heat_hbm.1) | copy-start | bytes 12292
  5.7 0.7 %copy-start.5 = (f32[1024]{0:T(1024)S(1)}, f32[1024]{0:T(1024)}, u32[]{:S(2)}) copy-start(f32[1024]{0:T(1024)} %diam_hbm.1) | copy-start | bytes 12292
  6.4 0.7 %copy-start.6 = (s32[1024]{0:T(1024)S(1)}, s32[1024]{0:T(1024)}, u32[]{:S(2)}) copy-start(s32[1024]{0:T(1024)} %li_hbm.1) | copy-start | bytes 12292
  7.0 0.7 %copy-start.7 = (s32[1024]{0:T(1024)S(1)}, s32[1024]{0:T(1024)}, u32[]{:S(2)}) copy-start(s32[1024]{0:T(1024)} %lj_hbm.1) | copy-start | bytes 12292
  7.7 0.7 %copy-start.8 = (s32[1024]{0:T(1024)S(1)}, s32[1024]{0:T(1024)}, u32[]{:S(2)}) copy-start(s32[1024]{0:T(1024)} %lk_hbm.1) | copy-start | bytes 12292

commit v2 on v1

--- a/solution.py
+++ b/solution.py
@@ -596,7 +596,7 @@
         compiler_params=pltpu.CompilerParams(
             collective_id=0, has_side_effects=True, vmem_limit_bytes=32 * 1024 * 1024
         ),
-    )(vel, scal, pos, mot, heat, diam, li, lj, lk, tally)
+    )(*(pltpu.with_memory_space_constraint(x, pltpu.HBM) for x in (vel, scal, pos, mot, heat, diam, li, lj, lk)), tally)
 
 
 def solution(mesh):

time: 41 us -> 33.6 us (0.82)
  local copies, waits for them, and re-layouts: 8.8 us -> 1.67 us
    unnamed x20 -> x2, local copies, waits for them, and re-layouts: 8.8 us -> 1.67 us
where the time goes in v2:
time: 33.6 us; the launch traced here: 33.5 us
  Pallas kernels  30.5 us (91%)
  local copies, waits for them, and re-layouts  1.67 us (5%)
  between operations  1.29 us (4%)
    pallas_call x1, Pallas kernels, local(): pl.pallas_call(functools.partial(kernel, sizes), out_shape=(jax.ShapeDtyp...  30.5 us
    unnamed x2, local copies, waits for them, and re-layouts  1.67 us

profile of v2, /device:TPU:71, one launch (start us, length us, event | category | flops | bytes accessed | tf_op | source)
XLA Modules:
  0.0 33.5 jit_solution(751064502214005301)
XLA Ops:
  1.3 30.5 %shard_map.113 = (f32[5,8,64,128]{3,2,1,0:T(8,128)S(1)}, f32[5,1024]{1,0:T(8,128)S(1)}) custom-call(f32[3,8,64,128]{3,2,1,0:T(8,128)} %vel.1, f32[3,8,64,128]{3,2,1,0:T(8,128)} %scal.1, f32[3,1024]{1,0:T(4,128)} %pos_hbm.1, f32[3,1024]{1,0:T(4,128)} %mot_hbm.1, f32[1024]{0:T(1024)} %heat_hbm.1, f32[1024]{0:T(1024)} %diam_hbm.1, s32[1024]{0:T(1024)} %li_hbm.1, ...), custom_call_target="tpu_custom_call" | custom-call | tf_op jit(solution)/shard_map/pallas_call | solution.py:542
  31.8 1.1 %copy.15 = f32[5,8,64,128]{3,2,1,0:T(8,128)} copy(f32[5,8,64,128]{3,2,1,0:T(8,128)S(1)} %get-tuple-element.4) | data formatting | bytes 2621440
  32.8 0.6 %copy.16 = f32[5,1024]{1,0:T(8,128)} copy(f32[5,1024]{1,0:T(8,128)S(1)} %get-tuple-element.5) | data formatting | bytes 40960

commit v3 on v2

--- a/solution.py
+++ b/solution.py
@@ -1,4 +1,5 @@
 import functools
+import itertools
 
 import jax
 import jax.numpy as jnp
@@ -72,6 +73,9 @@
     l_lo,
     u_hi,
     u_lo,
+    x_hi,
+    x_lo,
+    edges,
     ws,
     ws_ends,
     wi,
@@ -81,6 +85,7 @@
     part_out,
     part_in,
     terms_out,
+    terms_pack,
     terms_in,
     yb,
     y_out,
@@ -92,6 +97,12 @@
     dz_out,
     dz_in,
     dyz_in,
+    dxz_out,
+    dxz_in,
+    dxy_out,
+    dxy_in,
+    dxyz_in,
+    zt,
     local_sem,
     send_sem,
     recv_sem,
@@ -116,19 +127,28 @@
 
     numbers = iter(range(64))
 
+    def pack(ref, number, row):
+        for b in range(n // 128):
+            at = number * (n // 128) + b
+            ref[at : at + 1, :] = row[:, b * 128 : b * 128 + 128]
+
+    def unpack(ref, number):
+        first = number * (n // 128)
+        return jnp.concatenate([ref[first + b : first + b + 1, :] for b in range(n // 128)], axis=1)
+
     def both(axis, up, land0, down, land1):
         return (
             (next(numbers), ((axis, 1),), up, land0),
             (next(numbers), ((axis, -1),), down, land1),
         )
 
-    def corners(source, land):
+    def diagonal(axes, source, land):
         found = []
-        for y in (1, -1):
-            for z in (1, -1):
-                sides = (0 if y > 0 else 1, 0 if z > 0 else 1)
-                steps = (("gy", y), ("gz", z))
-                found.append((next(numbers), steps, source(1 - sides[1]), land.at[sides]))
+        for steps in itertools.product((1, -1), repeat=len(axes)):
+            sides = tuple((1 - step) // 2 for step in steps)
+            from_sides = tuple(1 - side for side in sides)
+            steps = tuple(zip(axes, steps))
+            found.append((next(numbers), steps, source(*from_sides), land.at[sides]))
         return tuple(found)
 
     def copy(transfer, steps):
@@ -162,12 +182,12 @@
             def _():
                 land[...] = jnp.zeros(land.shape, F32)
 
-    g_pos = both("gx", mine, theirs.at[0], mine, theirs.at[1])
+    g_pos = both("gx", mine.at[1], theirs.at[0], mine.at[0], theirs.at[1])
     g_y = both("gy", y_out.at[1], yb.at[:, 0:8], y_out.at[0], yb.at[:, 16:24])
     g_z = both("gz", z_out.at[1], z_in.at[0:8], z_out.at[0], z_in.at[8:16])
-    g_yz = corners(lambda side: z_out.at[side], yz_in)
+    g_yz = diagonal(("gy", "gz"), lambda y, z: z_out.at[z], yz_in)
     g_part = both("gx", part_out.at[1], part_in.at[0], part_out.at[0], part_in.at[1])
-    d_terms = both("gx", terms_out, terms_in.at[0], terms_out, terms_in.at[1])
+    d_terms = both("gx", terms_pack, terms_in.at[0], terms_pack, terms_in.at[1])
     d_z = both(
         "gz",
         dz_out.at[8:16, 0:OWN],
@@ -176,8 +196,20 @@
         dz_in.at[8:16],
     )
     d_y = both("gy", dy.at[16:24], dy_in.at[0], dy.at[0:8], dy_in.at[1])
-    d_yz = corners(lambda side: dz_out.at[8 * side : 8 * side + 8, OWN:COLS], dyz_in)
-    groups = (g_pos, g_y, g_z, g_yz, g_part, d_terms, d_z, d_y, d_yz)
+    d_yz = diagonal(
+        ("gy", "gz"), lambda y, z: dz_out.at[8 * z : 8 * z + 8, OWN:COLS], dyz_in
+    )
+    d_xz = diagonal(("gx", "gz"), lambda x, z: dxz_out.at[8 * z : 8 * z + 8], dxz_in)
+
+    def edge(x, y):
+        first = 16 * x + 8 * y
+        return slice(first, first + 8)
+
+    d_xy = diagonal(("gx", "gy"), lambda x, y: dxy_out.at[edge(x, y), 0:128], dxy_in)
+    d_xyz = diagonal(
+        ("gx", "gy", "gz"), lambda x, y, z: dxy_out.at[edge(x, y), 128:256], dxyz_in
+    )
+    groups = (g_pos, g_y, g_z, g_yz, g_part, d_terms, d_xz, d_xy, d_xyz, d_z, d_y, d_yz)
 
     loads = []
     for number, (source, land) in enumerate(
@@ -209,10 +241,8 @@
     yb[:, 8:16] = jnp.zeros((NF, 8, CK), F32)
     yb[:, 24:128] = jnp.zeros((NF, 104, CK), F32)
     z_out[...] = jnp.zeros(z_out.shape, F32)
-    part_out[:, 6:8] = jnp.zeros((2, 2, n), F32)
-    for x in range(2):
-        l_hi[x, CK : 2 * CK] = jnp.zeros((CK, n), BF16)
-        l_lo[x, CK : 2 * CK] = jnp.zeros((CK, n), BF16)
+    dxy_out[...] = jnp.zeros(dxy_out.shape, F32)
+    zt[...] = jnp.zeros(zt.shape, F32)
     s_hi[OWN + 32 : COLS] = jnp.zeros((96, n), BF16)
     s_lo[OWN + 32 : COLS] = jnp.zeros((96, n), BF16)
     t_hi[NS * CK + 16 :] = jnp.zeros((112, n), BF16)
@@ -220,10 +250,12 @@
 
     for load in loads[0:4]:
         load.wait()
-    mine[0:3] = pos[...]
-    for axis, cell in enumerate((li, lj, lk)):
-        mine[3 + axis : 4 + axis] = cell[...].reshape(1, n).astype(F32)
-    mine[6:8] = jnp.zeros((2, n), F32)
+    at = [pos[axis : axis + 1] for axis in range(3)]
+    cell = [ref[...].reshape(1, n).astype(F32) for ref in (li, lj, lk)]
+    reach = [tent(at[0] - (place - cell[0])) for place in (-1.0, float(CI))]
+    for x in range(2):
+        for number, row in enumerate((reach[x], at[1], cell[1], at[2], cell[2])):
+            pack(mine.at[x], number, row)
 
     near = {axis: jnp.minimum(me[axis], 1) + jnp.minimum(ends[axis] - me[axis], 1) for axis in axes}
     pl.semaphore_wait(barrier, near["gx"] + near["gy"] + near["gz"] + near["gy"] * near["gz"])
@@ -252,13 +284,22 @@
         return iota((rows, n), 0).astype(F32)
 
     row16 = iota((16, n), 0)
-    spread = tent(mine[0:1] - (ramp(16) - mine[3:4]))
-    wi[...] = jnp.where(row16 < CI, spread, 0.0)
-    wj = tent(mine[1:2] - (ramp(CJ) - mine[4:5]))
-    wj_ends = (tent(mine[1:2] - (-1.0 - mine[4:5])), tent(mine[1:2] - (float(CJ) - mine[4:5])))
-    lines[...] = tent(mine[2:3] - (ramp(CK) - mine[5:6]))
-    line_ends[0:1] = tent(mine[2:3] - (-1.0 - mine[5:6]))
-    line_ends[1:2] = tent(mine[2:3] - (float(CK) - mine[5:6]))
+
+    def k_weights(x, offset, cell):
+        hi, lo = split(tent(offset - (ramp(CK) - cell)))
+        l_hi[x, 0:CK] = hi
+        l_lo[x, 0:CK] = lo
+        low, high = tent(offset - (-1.0 - cell)), tent(offset - (float(CK) - cell))
+        hi, lo = split(jnp.where(row16 == 0, low, jnp.where(row16 == 8, high, 0.0)))
+        l_hi[x, CK:] = hi
+        l_lo[x, CK:] = lo
+        return low, high
+
+    wi[...] = jnp.where(row16 < CI, tent(at[0] - (ramp(16) - cell[0])), 0.0)
+    wj = tent(at[1] - (ramp(CJ) - cell[1]))
+    wj_ends = (tent(at[1] - (-1.0 - cell[1])), tent(at[1] - (float(CJ) - cell[1])))
+    lines[...] = tent(at[2] - (ramp(CK) - cell[2]))
+    line_ends[0:1], line_ends[1:2] = k_weights(2, at[2], cell[2])
     for i in range(CI):
         hi, lo = split(wi[i : i + 1] * wj)
         s_hi[i * CJ : i * CJ + CJ] = hi
@@ -267,6 +308,12 @@
         hi, lo = split(wi[...] * wj_ends[y])
         s_hi[OWN + 16 * y : OWN + 16 * y + 16] = hi
         s_lo[OWN + 16 * y : OWN + 16 * y + 16] = lo
+    for x in range(2):
+        hi, lo = split(reach[x] * wj)
+        x_hi[x * CJ : x * CJ + CJ] = hi
+        x_lo[x * CJ : x * CJ + CJ] = lo
+        for y in range(2):
+            edges[2 * x + y : 2 * x + y + 1] = reach[x] * wj_ends[y]
 
     lane16 = iota((16, 128), 1)
     arrive(g_y)
@@ -350,23 +397,15 @@
 
     arrive(g_pos)
     for x in range(2):
-        p = theirs.at[x]
-        reach = tent(p[0:1] - ((float(CI) if x == 0 else -1.0) - p[3:4]))
-        ws[x] = reach * tent(p[1:2] - (ramp(CJ) - p[4:5]))
-        ws_ends[x, 0:1] = reach * tent(p[1:2] - (-1.0 - p[4:5]))
-        ws_ends[x, 1:2] = reach * tent(p[1:2] - (float(CJ) - p[4:5]))
-        hi, lo = split(tent(p[2:3] - (ramp(CK) - p[5:6])))
-        l_hi[x, 0:CK] = hi
-        l_lo[x, 0:CK] = lo
-        low = tent(p[2:3] - (-1.0 - p[5:6]))
-        high = tent(p[2:3] - (float(CK) - p[5:6]))
-        hi, lo = split(jnp.where(row16 == 0, low, jnp.where(row16 == 8, high, 0.0)))
-        l_hi[x, CK : CK + 16] = hi
-        l_lo[x, CK : CK + 16] = lo
+        near_x, at_j, cell_j, at_k, cell_k = [unpack(theirs.at[x], q) for q in range(5)]
+        ws[x] = near_x * tent(at_j - (ramp(CJ) - cell_j))
+        ws_ends[x, 0:1] = near_x * tent(at_j - (-1.0 - cell_j))
+        ws_ends[x, 1:2] = near_x * tent(at_j - (float(CJ) - cell_j))
+        k_weights(x, at_k, cell_k)
     for x in range(2):
         for chunk in chunks:
             top, low = l_hi[x, 0:CK, chunk], l_lo[x, 0:CK, chunk]
-            top_z, low_z = l_hi[x, CK : CK + 16, chunk], l_lo[x, CK : CK + 16, chunk]
+            top_z, low_z = l_hi[x, CK:, chunk], l_lo[x, CK:, chunk]
             right = jnp.concatenate(
                 [top, low, top, top_z, low_z, top_z, jnp.zeros((80, 256), BF16)], axis=0
             )
@@ -377,7 +416,10 @@
             weight = ws[x, :, chunk]
             for f in range(NF):
                 row = jnp.sum(value[f * CJ : f * CJ + CJ] * weight, axis=0, keepdims=True)
-                part_out[x, f : f + 1, chunk] = row + total[f : f + 1]
+                row = row + total[f : f + 1]
+                for b in range(2):
+                    put = f * (n // 128) + chunk.start // 128 + b
+                    part_out[x, put : put + 1, :] = row[:, b * 128 : b * 128 + 128]
     send(g_part)
 
     for chunk in chunks[2:]:
@@ -388,9 +430,12 @@
     q = diam[...].reshape(1, n)
     live = iota((1, n), 1) // TILE < tally[0]
     arrive(g_part)
-    got = gathered[0:NF] + part_in[0, 0:NF] + part_in[1, 0:NF]
-    gas = got[0:3]
-    gas_heat, moisture, rho = got[3:4], got[4:5], got[5:6]
+    got = [
+        gathered[f : f + 1] + unpack(part_in.at[0], f) + unpack(part_in.at[1], f)
+        for f in range(NF)
+    ]
+    gas = jnp.concatenate(got[0:3], axis=0)
+    gas_heat, moisture, rho = got[3:6]
     drag = step_time / (0.5 * q)
     new_motion = (motion + drag * gas) / (1.0 + drag)
     mass = q * jnp.sqrt(q)
@@ -409,23 +454,42 @@
     terms_out[3:4] = jnp.where(live, mass * (warmth - new_heat), 0.0)
     terms_out[4:5] = jnp.where(live, mass - new_mass, 0.0)
     terms_out[5:8] = jnp.zeros((3, n), F32)
+    for c in range(NS):
+        pack(terms_pack, c, terms_out[c : c + 1])
     send(d_terms)
+
+    def cross(left, right):
+        return lax.dot_general(
+            left, right, (((1,), (1,)), ((), ())), preferred_element_type=F32
+        )
+
+    tail = jnp.concatenate(
+        [terms_out[...] * line_ends[0:1], terms_out[...] * line_ends[1:2]], axis=0
+    )
+    hi, lo = split(tail)
+    t_hi[NS * CK : NS * CK + 16] = hi
+    t_lo[NS * CK : NS * CK + 16] = lo
+    left = jnp.concatenate([x_hi[...], x_lo[...], x_hi[...]], axis=1)
+    right = jnp.concatenate(
+        [jnp.concatenate([hi, hi, lo], axis=1), jnp.zeros((112, 3 * n), BF16)], axis=0
+    )
+    dxz_out[...] = cross(left, right).T[0:16]
+    hi, lo = split(
+        jnp.concatenate([terms_out[...] * edges[line : line + 1] for line in range(4)], axis=0)
+    )
+    left = jnp.concatenate([hi, hi, lo], axis=1)
+    right = jnp.concatenate([l_hi[2], l_lo[2], l_hi[2]], axis=1)
+    value = cross(left, right)
+    dxy_out[:, 0:128] = value[:, 0:CK]
+    dxy_out[:, 128:144] = value[:, CK : CK + 16]
+    send(d_xyz)
+    send(d_xy)
+    send(d_xz)
 
     for c in range(NS):
         hi, lo = split(terms_out[c : c + 1] * lines[...])
         t_hi[c * CK : c * CK + CK] = hi
         t_lo[c * CK : c * CK + CK] = lo
-    tail = jnp.concatenate(
-        [terms_out[...] * line_ends[0:1], terms_out[...] * line_ends[1:2]], axis=0
-    )
-    hi, lo = split(tail)
-    t_hi[NS * CK : NS * CK + 16] = hi
-    t_lo[NS * CK : NS * CK + 16] = lo
-
-    def cross(left, right):
-        return lax.dot_general(
-            left, right, (((1,), (1,)), ((), ())), preferred_element_type=F32
-        )
 
     lines_used = slice(0, OWN + 32)
     for w in range(3):
@@ -447,63 +511,32 @@
                 rest = jnp.concatenate([half[OWN : OWN + 32], jnp.zeros((96, 128), F32)], axis=0)
                 dz_out[:, OWN:COLS] = rest.T[0:16]
 
+    send(d_z)
+    send(d_yz)
+    send(d_y)
+
     arrive(d_terms)
-    lane1 = iota((1, 128), 1)
     for x in range(2):
         i = 0 if x == 0 else CI - 1
         weight = ws[x]
         for c in range(NS):
-            hi, lo = split(terms_in[x, c : c + 1] * weight)
+            hi, lo = split(unpack(terms_in.at[x], c) * weight)
             u_hi[c * CJ : c * CJ + CJ] = hi
             u_lo[c * CJ : c * CJ + CJ] = lo
-        last = NS * CJ
-        for y in range(2):
-            hi, lo = split(
-                jnp.concatenate(
-                    [terms_in[x] * ws_ends[x, y : y + 1], jnp.zeros((8, n), F32)], axis=0
-                )
-            )
-            u_hi[last + 16 * y : last + 16 * y + 16] = hi
-            u_lo[last + 16 * y : last + 16 * y + 16] = lo
         left = jnp.concatenate([u_hi[...], u_hi[...], u_lo[...]], axis=1)
-        right = jnp.concatenate([l_hi[x], l_lo[x], l_hi[x]], axis=1)
+        right = jnp.concatenate([l_hi[x, 0:CK], l_lo[x, 0:CK], l_hi[x, 0:CK]], axis=1)
         value = cross(left, right)
         for c in range(NS):
-            out[c, i] = out[c, i] + value[c * CJ : c * CJ + CJ, 0:CK]
-            for y in range(2):
-                row = 16 * y + i
-                at = slice(c * CK, c * CK + CK)
-                line = last + 16 * y + c
-                dy[row : row + 1, at] = dy[row : row + 1, at] + value[line : line + 1, 0:CK]
-        first = i * CJ // 128 * 128
-        keep = lane1 < CJ if x == 0 else lane1 >= CJ
-        for b in range(3):
-            block = value[b * 128 : min(b * 128 + 128, last + 32), CK : 2 * CK]
-            if b == 2:
-                block = jnp.concatenate([block, jnp.zeros((32, 128), F32)], axis=0)
-            block = block.T
-            for c in range(2 * b, min(2 * b + 2, NS)):
-                for z in range(2):
-                    row = block[8 * z : 8 * z + 1]
-                    if c % 2 != x:
-                        row = pltpu.roll(row, CJ, 1)
-                    at = 8 * z + c
-                    old = dz_out[at : at + 1, first : first + 128]
-                    dz_out[at : at + 1, first : first + 128] = old + jnp.where(keep, row, 0.0)
-        for y in range(2):
-            block = value[last + 16 * y : last + 16 * y + 8, CK : 2 * CK]
-            to = 16 * y + i
-            for z in range(2):
-                moved = pltpu.roll(block, (to - 8 * z) % 128, 1)
-                old = dz_out[8 * z : 8 * z + 8, OWN:COLS]
-                dz_out[8 * z : 8 * z + 8, OWN:COLS] = old + jnp.where(lane8 == to, moved, 0.0)
-    send(d_z)
-    send(d_yz)
-    send(d_y)
-
+            out[c, i] = out[c, i] + value[c * CJ : c * CJ + CJ]
+
+    arrive(d_z)
+    arrive(d_y)
     arrive(d_yz)
-    arrive(d_z)
+    arrive(d_xz)
+    arrive(d_xy)
+    arrive(d_xyz)
     lane128 = iota((128, 128), 1)
+    rim = (lane128 == 0) | (lane128 == CK - 1)
     for b in range(OWN // 128):
         block = dz_in[:, b * 128 : b * 128 + 128]
         for i in (2 * b, 2 * b + 1):
@@ -513,22 +546,36 @@
                 moved = jnp.concatenate([dyz_in[y, 0], dyz_in[y, 1]], axis=0)
                 moved = pltpu.roll(moved, (to - at) % 128, 1)
                 block = block + jnp.where(lane16 == to, moved, 0.0)
-        columns = jnp.concatenate([block, jnp.zeros((112, 128), F32)], axis=0).T
+        if b in (0, OWN // 128 - 1):
+            x = 0 if b == 0 else 1
+            moved = jnp.concatenate([dxz_in[x, 0], dxz_in[x, 1]], axis=0)
+            half = lane16 < CJ if x == 0 else lane16 >= CJ
+            block = block + jnp.where(half, pltpu.roll(moved, CJ, 1), 0.0)
+            for y in range(2):
+                to = CJ * x + (0 if y == 0 else CJ - 1)
+                moved = jnp.concatenate(
+                    [
+                        pltpu.roll(dxyz_in[x, y, z], (to - 8 * (1 - z)) % 128, 1)
+                        for z in range(2)
+                    ],
+                    axis=0,
+                )
+                block = block + jnp.where(lane16 == to, moved, 0.0)
         for c in range(NS):
-            add = jnp.where(
-                lane128 == 0,
-                columns[:, c : c + 1],
-                jnp.where(lane128 == CK - 1, columns[:, 8 + c : 9 + c], 0.0),
-            ).reshape(2, CJ, CK)
-            out[c, 2 * b : 2 * b + 2] = out[c, 2 * b : 2 * b + 2] + add
-    arrive(d_y)
+            zt[b, 2 * c : 2 * c + 1] = block[8 + c : 9 + c]
+            zt[b, 2 * c + 1 : 2 * c + 2] = block[c : c + 1]
+        columns = jnp.concatenate([zt[b], jnp.zeros((112, 128), F32)], axis=0).T
+        for c in range(NS):
+            add = jnp.where(rim, pltpu.roll(columns, 127 - 2 * c, 1), 0.0)
+            out[c, 2 * b : 2 * b + 2] = out[c, 2 * b : 2 * b + 2] + add.reshape(2, CJ, CK)
     for y in range(2):
         j = 0 if y == 0 else CJ - 1
         for c in range(NS):
             for i in range(CI):
-                out[c, i, j : j + 1, :] = (
-                    out[c, i, j : j + 1, :] + dy_in[y, i : i + 1, c * CK : c * CK + CK]
-                )
+                add = dy_in[y, i : i + 1, c * CK : c * CK + CK]
+                if i in (0, CI - 1):
+                    add = add + dxy_in[0 if i == 0 else 1, y, c : c + 1, :]
+                out[c, i, j : j + 1, :] = out[c, i, j : j + 1, :] + add
 
     for group in groups:
         sent(group)
@@ -556,8 +603,8 @@
             pltpu.VMEM((n,), jnp.int32),
             pltpu.VMEM((n,), jnp.int32),
             pltpu.VMEM((n,), jnp.int32),
-            pltpu.VMEM((8, n), F32),
-            pltpu.VMEM((2, 8, n), F32),
+            pltpu.VMEM((2, 5 * n // 128, 128), F32),
+            pltpu.VMEM((2, 5 * n // 128, 128), F32),
             pltpu.VMEM((ROWS, COLS), BF16),
             pltpu.VMEM((ROWS, COLS), BF16),
             pltpu.VMEM((COLS, n), BF16),
@@ -565,20 +612,24 @@
             pltpu.VMEM((768, n), BF16),
             pltpu.VMEM((768, n), BF16),
             pltpu.VMEM((2, planes, 512), BF16),
-            pltpu.VMEM((2, 2 * CK, n), BF16),
-            pltpu.VMEM((2, 2 * CK, n), BF16),
-            pltpu.VMEM((NS * CJ + 32, n), BF16),
-            pltpu.VMEM((NS * CJ + 32, n), BF16),
+            pltpu.VMEM((3, CK + 16, n), BF16),
+            pltpu.VMEM((3, CK + 16, n), BF16),
+            pltpu.VMEM((NS * CJ, n), BF16),
+            pltpu.VMEM((NS * CJ, n), BF16),
+            pltpu.VMEM((2 * CJ, n), BF16),
+            pltpu.VMEM((2 * CJ, n), BF16),
+            pltpu.VMEM((8, n), F32),
             pltpu.VMEM((2, CJ, n), F32),
             pltpu.VMEM((2, 8, n), F32),
             pltpu.VMEM((16, n), F32),
             pltpu.VMEM((CK, n), F32),
             pltpu.VMEM((8, n), F32),
             pltpu.VMEM((8, n), F32),
-            pltpu.VMEM((2, 8, n), F32),
-            pltpu.VMEM((2, 8, n), F32),
+            pltpu.VMEM((2, NF * n // 128, 128), F32),
+            pltpu.VMEM((2, NF * n // 128, 128), F32),
             pltpu.VMEM((8, n), F32),
-            pltpu.VMEM((2, 8, n), F32),
+            pltpu.VMEM((NS * n // 128, 128), F32),
+            pltpu.VMEM((2, NS * n // 128, 128), F32),
             pltpu.VMEM((NF, 128, CK), F32),
             pltpu.VMEM((2, NF, 8, CK), F32),
             pltpu.VMEM((2, 8, OWN), F32),
@@ -589,9 +640,15 @@
             pltpu.VMEM((16, COLS), F32),
             pltpu.VMEM((16, OWN), F32),
             pltpu.VMEM((2, 2, 8, 128), F32),
+            pltpu.VMEM((16, 128), F32),
+            pltpu.VMEM((2, 2, 8, 128), F32),
+            pltpu.VMEM((32, 256), F32),
+            pltpu.VMEM((2, 2, 8, 128), F32),
+            pltpu.VMEM((2, 2, 2, 8, 128), F32),
+            pltpu.VMEM((OWN // 128, 16, 128), F32),
             pltpu.SemaphoreType.DMA((9,)),
-            pltpu.SemaphoreType.DMA((22,)),
-            pltpu.SemaphoreType.DMA((22,)),
+            pltpu.SemaphoreType.DMA((38,)),
+            pltpu.SemaphoreType.DMA((38,)),
         ],
         compiler_params=pltpu.CompilerParams(
             collective_id=0, has_side_effects=True, vmem_limit_bytes=32 * 1024 * 1024

time: 33.6 us -> 29.4 us (0.87)
  Pallas kernels: 30.5 us -> 26.3 us
    pallas_call x1, Pallas kernels: 30.5 us -> 26.3 us  [local(): pl.pallas_call(functools.partial(kernel, sizes), out_shape=(jax.ShapeDtyp...]
where the time goes in v3:
time: 29.4 us; the launch traced here: 29.3 us
  Pallas kernels  26.3 us (89%)
  local copies, waits for them, and re-layouts  1.67 us (6%)
  between operations  1.29 us (4%)
    pallas_call x1, Pallas kernels, local(): pl.pallas_call(functools.partial(kernel, sizes), out_shape=(jax.ShapeDtyp...  26.3 us
    unnamed x2, local copies, waits for them, and re-layouts  1.67 us

profile of v3, /device:TPU:71, one launch (start us, length us, event | category | flops | bytes accessed | tf_op | source)
XLA Modules:
  0.0 29.3 jit_solution(11390628472625039231)
XLA Ops:
  1.3 26.3 %shard_map.113 = (f32[5,8,64,128]{3,2,1,0:T(8,128)S(1)}, f32[5,1024]{1,0:T(8,128)S(1)}) custom-call(f32[3,8,64,128]{3,2,1,0:T(8,128)} %vel.1, f32[3,8,64,128]{3,2,1,0:T(8,128)} %scal.1, f32[3,1024]{1,0:T(4,128)} %pos_hbm.1, f32[3,1024]{1,0:T(4,128)} %mot_hbm.1, f32[1024]{0:T(1024)} %heat_hbm.1, f32[1024]{0:T(1024)} %diam_hbm.1, s32[1024]{0:T(1024)} %li_hbm.1, ...), custom_call_target="tpu_custom_call" | custom-call | tf_op jit(solution)/shard_map/pallas_call | solution.py:589
  27.6 1.1 %copy.15 = f32[5,8,64,128]{3,2,1,0:T(8,128)} copy(f32[5,8,64,128]{3,2,1,0:T(8,128)S(1)} %get-tuple-element.4) | data formatting | bytes 2621440
  28.6 0.6 %copy.16 = f32[5,1024]{1,0:T(8,128)} copy(f32[5,1024]{1,0:T(8,128)S(1)} %get-tuple-element.5) | data formatting | bytes 40960

commit v4 on v3

--- a/solution.py
+++ b/solution.py
@@ -52,6 +52,8 @@
     tally,
     out,
     state,
+    zt,
+    rows,
     fields,
     pos,
     mot,
@@ -102,7 +104,6 @@
     dxy_out,
     dxy_in,
     dxyz_in,
-    zt,
     local_sem,
     send_sem,
     recv_sem,
@@ -211,6 +212,14 @@
     )
     groups = (g_pos, g_y, g_z, g_yz, g_part, d_terms, d_xz, d_xy, d_xyz, d_z, d_y, d_yz)
 
+    barrier = pltpu.get_barrier_semaphore()
+    for _, steps, _, _ in g_pos + g_y + g_z + g_yz:
+        pl.when(there(steps))(
+            lambda s=steps: pl.semaphore_signal(
+                barrier, inc=1, device_id=peer(s), device_id_type=MESH
+            )
+        )
+
     loads = []
     for number, (source, land) in enumerate(
         (
@@ -228,21 +237,13 @@
         loads.append(pltpu.make_async_copy(source, land, local_sem.at[number]))
         loads[-1].start()
 
-    barrier = pltpu.get_barrier_semaphore()
-    for _, steps, _, _ in g_pos + g_y + g_z + g_yz:
-        pl.when(there(steps))(
-            lambda s=steps: pl.semaphore_signal(
-                barrier, inc=1, device_id=peer(s), device_id_type=MESH
-            )
-        )
-
     for group in groups:
         blank(group)
     yb[:, 8:16] = jnp.zeros((NF, 8, CK), F32)
     yb[:, 24:128] = jnp.zeros((NF, 104, CK), F32)
     z_out[...] = jnp.zeros(z_out.shape, F32)
     dxy_out[...] = jnp.zeros(dxy_out.shape, F32)
-    zt[...] = jnp.zeros(zt.shape, F32)
+    zt[:, 10:16] = jnp.zeros((OWN // 128, 6, 128), F32)
     s_hi[OWN + 32 : COLS] = jnp.zeros((96, n), BF16)
     s_lo[OWN + 32 : COLS] = jnp.zeros((96, n), BF16)
     t_hi[NS * CK + 16 :] = jnp.zeros((112, n), BF16)
@@ -257,18 +258,12 @@
         for number, row in enumerate((reach[x], at[1], cell[1], at[2], cell[2])):
             pack(mine.at[x], number, row)
 
-    near = {axis: jnp.minimum(me[axis], 1) + jnp.minimum(ends[axis] - me[axis], 1) for axis in axes}
-    pl.semaphore_wait(barrier, near["gx"] + near["gy"] + near["gz"] + near["gy"] * near["gz"])
-    send(g_pos)
-
     for load in loads[4:]:
         load.wait()
     for f in range(NF):
         for i in range(CI):
             y_out[0, f, i : i + 1, :] = fields[f, i, 0:1, :]
             y_out[1, f, i : i + 1, :] = fields[f, i, CJ - 1 : CJ, :]
-    send(g_y)
-
     for f in range(NF):
         for b in range(OWN // 128):
             block = fields[f, 2 * b : 2 * b + 2].reshape(128, CK).T
@@ -277,6 +272,11 @@
             hi, lo = split(block)
             a_hi[f * CK : f * CK + CK, b * 128 : b * 128 + 128] = hi
             a_lo[f * CK : f * CK + CK, b * 128 : b * 128 + 128] = lo
+    near = {axis: jnp.minimum(me[axis], 1) + jnp.minimum(ends[axis] - me[axis], 1) for axis in axes}
+    pl.semaphore_wait(barrier, near["gx"] + near["gy"] + near["gz"] + near["gy"] * near["gz"])
+    send(g_pos)
+
+    send(g_y)
     send(g_z)
     send(g_yz)
 
@@ -515,28 +515,30 @@
     send(d_yz)
     send(d_y)
 
+    for group in (g_pos, g_y, g_z, g_yz, g_part):
+        sent(group)
     arrive(d_terms)
     for x in range(2):
         i = 0 if x == 0 else CI - 1
         weight = ws[x]
         for c in range(NS):
             hi, lo = split(unpack(terms_in.at[x], c) * weight)
-            u_hi[c * CJ : c * CJ + CJ] = hi
-            u_lo[c * CJ : c * CJ + CJ] = lo
-        left = jnp.concatenate([u_hi[...], u_hi[...], u_lo[...]], axis=1)
+            u_hi[x, c * CJ : c * CJ + CJ] = hi
+            u_lo[x, c * CJ : c * CJ + CJ] = lo
+        left = jnp.concatenate([u_hi[x], u_hi[x], u_lo[x]], axis=1)
         right = jnp.concatenate([l_hi[x, 0:CK], l_lo[x, 0:CK], l_hi[x, 0:CK]], axis=1)
         value = cross(left, right)
         for c in range(NS):
             out[c, i] = out[c, i] + value[c * CJ : c * CJ + CJ]
 
+    for group in (d_terms, d_xz, d_xy, d_xyz):
+        sent(group)
     arrive(d_z)
     arrive(d_y)
     arrive(d_yz)
     arrive(d_xz)
     arrive(d_xy)
     arrive(d_xyz)
-    lane128 = iota((128, 128), 1)
-    rim = (lane128 == 0) | (lane128 == CK - 1)
     for b in range(OWN // 128):
         block = dz_in[:, b * 128 : b * 128 + 128]
         for i in (2 * b, 2 * b + 1):
@@ -564,21 +566,42 @@
         for c in range(NS):
             zt[b, 2 * c : 2 * c + 1] = block[8 + c : 9 + c]
             zt[b, 2 * c + 1 : 2 * c + 2] = block[c : c + 1]
-        columns = jnp.concatenate([zt[b], jnp.zeros((112, 128), F32)], axis=0).T
-        for c in range(NS):
-            add = jnp.where(rim, pltpu.roll(columns, 127 - 2 * c, 1), 0.0)
-            out[c, 2 * b : 2 * b + 2] = out[c, 2 * b : 2 * b + 2] + add.reshape(2, CJ, CK)
-    for y in range(2):
-        j = 0 if y == 0 else CJ - 1
-        for c in range(NS):
+    rows[...] = dy_in[...]
+    for x in range(2):
+        i = 0 if x == 0 else CI - 1
+        for y in range(2):
+            for c in range(NS):
+                at = slice(c * CK, c * CK + CK)
+                rows[y, i : i + 1, at] = rows[y, i : i + 1, at] + dxy_in[x, y, c : c + 1, :]
+
+    for group in (d_z, d_y, d_yz):
+        sent(group)
+
+
+def deliver(part, state, zt, rows, out, state_out, whole, sem):
+    state_copy = pltpu.make_async_copy(state, state_out, sem.at[NS])
+    state_copy.start()
+    lane = iota((128, 128), 1)
+    rim = (lane == 0) | (lane == CK - 1)
+    blocks = range(OWN // 128)
+    columns = [
+        jnp.concatenate([zt[b], jnp.zeros((112, 128), F32)], axis=0).T for b in blocks
+    ]
+    copies = []
+    for c in range(NS):
+        for b in blocks:
+            add = jnp.where(rim, pltpu.roll(columns[b], 127 - 2 * c, 1), 0.0)
+            whole[c, 2 * b : 2 * b + 2] = part[c, 2 * b : 2 * b + 2] + add.reshape(2, CJ, CK)
+        for y in range(2):
+            j = 0 if y == 0 else CJ - 1
             for i in range(CI):
-                add = dy_in[y, i : i + 1, c * CK : c * CK + CK]
-                if i in (0, CI - 1):
-                    add = add + dxy_in[0 if i == 0 else 1, y, c : c + 1, :]
-                out[c, i, j : j + 1, :] = out[c, i, j : j + 1, :] + add
-
-    for group in groups:
-        sent(group)
+                whole[c, i, j : j + 1, :] = (
+                    whole[c, i, j : j + 1, :] + rows[y, i : i + 1, c * CK : c * CK + CK]
+                )
+        copies.append(pltpu.make_async_copy(whole.at[c], out.at[c], sem.at[c]))
+        copies[-1].start()
+    for copy in copies + [state_copy]:
+        copy.wait()
 
 
 def local(sizes, vel, scal, pos, mot, heat, diam, li, lj, lk, tally):
@@ -586,14 +609,16 @@
     vmem = pl.BlockSpec(memory_space=pltpu.VMEM)
     hbm = pl.BlockSpec(memory_space=pltpu.HBM)
     planes = NF * CJ + 16
-    return pl.pallas_call(
+    parts = pl.pallas_call(
         functools.partial(kernel, sizes),
         out_shape=(
             jax.ShapeDtypeStruct((NS, CI, CJ, CK), F32),
             jax.ShapeDtypeStruct((NS, n), F32),
+            jax.ShapeDtypeStruct((OWN // 128, 16, 128), F32),
+            jax.ShapeDtypeStruct((2, 8, NS * CK), F32),
         ),
         in_specs=[hbm] * 9 + [pl.BlockSpec(memory_space=pltpu.SMEM)],
-        out_specs=(vmem, vmem),
+        out_specs=(vmem,) * 4,
         scratch_shapes=[
             pltpu.VMEM((NF, CI, CJ, CK), F32),
             pltpu.VMEM((3, n), F32),
@@ -614,8 +639,8 @@
             pltpu.VMEM((2, planes, 512), BF16),
             pltpu.VMEM((3, CK + 16, n), BF16),
             pltpu.VMEM((3, CK + 16, n), BF16),
-            pltpu.VMEM((NS * CJ, n), BF16),
-            pltpu.VMEM((NS * CJ, n), BF16),
+            pltpu.VMEM((2, NS * CJ, n), BF16),
+            pltpu.VMEM((2, NS * CJ, n), BF16),
             pltpu.VMEM((2 * CJ, n), BF16),
             pltpu.VMEM((2 * CJ, n), BF16),
             pltpu.VMEM((8, n), F32),
@@ -645,7 +670,6 @@
             pltpu.VMEM((32, 256), F32),
             pltpu.VMEM((2, 2, 8, 128), F32),
             pltpu.VMEM((2, 2, 2, 8, 128), F32),
-            pltpu.VMEM((OWN // 128, 16, 128), F32),
             pltpu.SemaphoreType.DMA((9,)),
             pltpu.SemaphoreType.DMA((38,)),
             pltpu.SemaphoreType.DMA((38,)),
@@ -654,6 +678,17 @@
             collective_id=0, has_side_effects=True, vmem_limit_bytes=32 * 1024 * 1024
         ),
     )(*(pltpu.with_memory_space_constraint(x, pltpu.HBM) for x in (vel, scal, pos, mot, heat, diam, li, lj, lk)), tally)
+    return pl.pallas_call(
+        deliver,
+        out_shape=tuple(jax.ShapeDtypeStruct(part.shape, F32) for part in parts[:2]),
+        in_specs=[vmem] * 4,
+        out_specs=(hbm, hbm),
+        scratch_shapes=[
+            pltpu.VMEM((NS, CI, CJ, CK), F32),
+            pltpu.SemaphoreType.DMA((NS + 1,)),
+        ],
+        compiler_params=pltpu.CompilerParams(vmem_limit_bytes=4 * 1024 * 1024),
+    )(*parts)
 
 
 def solution(mesh):

time: 29.4 us -> 27.9 us (0.949)
  local copies, waits for them, and re-layouts: 1.67 us -> 0 us
    unnamed x2 -> x0, local copies, waits for them, and re-layouts: 1.67 us -> none
    pallas_call x0 -> x1, Pallas kernels: none -> 1.34 us  [local(): pl.pallas_call(deliver, out_shape=tuple((jax.ShapeDtypeStruct(part.shape,...]
    pallas_call x1, Pallas kernels: 26.3 us -> 25.1 us  [local(): pl.pallas_call(functools.partial(kernel, sizes), out_shape=(jax.ShapeDtyp...]
where the time goes in v4:
time: 27.9 us; the launch traced here: 27.8 us
  Pallas kernels  26.5 us (95%)
  between operations  1.29 us (5%)
    pallas_call x1, Pallas kernels, local(): pl.pallas_call(functools.partial(kernel, sizes), out_shape=(jax.ShapeDtyp...  25.1 us
    pallas_call x1, Pallas kernels, local(): pl.pallas_call(deliver, out_shape=tuple((jax.ShapeDtypeStruct(part.shape,...  1.34 us

profile of v4, /device:TPU:71, one launch (start us, length us, event | category | flops | bytes accessed | tf_op | source)
XLA Modules:
  0.0 27.8 jit_solution(6294086559090686009)
XLA Ops:
  1.3 25.1 %shard_map.113 = (f32[5,8,64,128]{3,2,1,0:T(8,128)S(1)}, f32[5,1024]{1,0:T(8,128)S(1)}, f32[4,16,128]{2,1,0:T(8,128)S(1)}, f32[2,8,640]{2,1,0:T(8,128)S(1)}) custom-call(f32[3,8,64,128]{3,2,1,0:T(8,128)} %vel.1, f32[3,8,64,128]{3,2,1,0:T(8,128)} %scal.1, f32[3,1024]{1,0:T(4,128)} %pos_hbm.1, f32[3,1024]{1,0:T(4,128)} %mot_hbm.1, f32[1024]{0:T(1024)} %heat_hbm.1, ...), custom_call_target="tpu_custom_call" | custom-call | tf_op jit(solution)/shard_map/pallas_call | solution.py:612
  26.4 1.3 %shard_map.114 = (f32[5,8,64,128]{3,2,1,0:T(8,128)}, f32[5,1024]{1,0:T(8,128)}) custom-call(f32[5,8,64,128]{3,2,1,0:T(8,128)S(1)} %get-tuple-element.6.part, f32[5,1024]{1,0:T(8,128)S(1)} %get-tuple-element.7.state, f32[4,16,128]{2,1,0:T(8,128)S(1)} %get-tuple-element.8.zt, f32[2,8,640]{2,1,0:T(8,128)S(1)} %get-tuple-element.9.rows), custom_call_target="tpu_custom_call" | custom-call | tf_op jit(solution)/shard_map/pallas_call | solution.py:681

commit v5 on v4

--- a/solution.py
+++ b/solution.py
@@ -15,6 +15,7 @@
 OWN = CI * CJ
 COLS = OWN + 128
 ROWS = NF * CK + 16
+PARTS = 1
 MESH = pl.DeviceIdType.MESH
 F32 = jnp.float32
 BF16 = jnp.bfloat16
@@ -68,13 +69,9 @@
     a_lo,
     s_hi,
     s_lo,
-    t_hi,
-    t_lo,
     e_lhs,
     l_hi,
     l_lo,
-    u_hi,
-    u_lo,
     x_hi,
     x_lo,
     edges,
@@ -104,11 +101,13 @@
     dxy_out,
     dxy_in,
     dxyz_in,
-    local_sem,
     send_sem,
     recv_sem,
 ):
     n = pos.shape[1]
+    width = n // PARTS
+    parts = [slice(h * width, h * width + width) for h in range(PARTS)]
+    per_row = width // 128
     axes = tuple(sizes)
     me = {axis: lax.axis_index(axis) for axis in axes}
     ends = {axis: size - 1 for axis, size in sizes.items()}
@@ -128,28 +127,37 @@
 
     numbers = iter(range(64))
 
-    def pack(ref, number, row):
-        for b in range(n // 128):
-            at = number * (n // 128) + b
+    def pack(ref, number, row, first=0):
+        for b in range(row.shape[1] // 128):
+            at = number * per_row + first + b
             ref[at : at + 1, :] = row[:, b * 128 : b * 128 + 128]
 
     def unpack(ref, number):
-        first = number * (n // 128)
-        return jnp.concatenate([ref[first + b : first + b + 1, :] for b in range(n // 128)], axis=1)
-
-    def both(axis, up, land0, down, land1):
+        first = number * per_row
+        return jnp.concatenate([ref[first + b : first + b + 1, :] for b in range(per_row)], axis=1)
+
+    def numbered(first, again):
+        send_number = iter(range(first, 64))
+        if again is not None:
+            taken = [transfer[0][1] for transfer in again]
+            return zip(send_number, taken)
+        return zip(send_number, numbers)
+
+    def both(first, axis, up, land0, down, land1, again=None):
+        pair = numbered(first, again)
         return (
-            (next(numbers), ((axis, 1),), up, land0),
-            (next(numbers), ((axis, -1),), down, land1),
-        )
-
-    def diagonal(axes, source, land):
+            (next(pair), ((axis, 1),), up, land0),
+            (next(pair), ((axis, -1),), down, land1),
+        )
+
+    def diagonal(first, axes, source, land):
         found = []
+        pair = numbered(first, None)
         for steps in itertools.product((1, -1), repeat=len(axes)):
             sides = tuple((1 - step) // 2 for step in steps)
             from_sides = tuple(1 - side for side in sides)
             steps = tuple(zip(axes, steps))
-            found.append((next(numbers), steps, source(*from_sides), land.at[sides]))
+            found.append((next(pair), steps, source(*from_sides), land.at[sides]))
         return tuple(found)
 
     def copy(transfer, steps):
@@ -157,8 +165,8 @@
         return pltpu.make_async_remote_copy(
             src_ref=source,
             dst_ref=land,
-            send_sem=send_sem.at[number],
-            recv_sem=recv_sem.at[number],
+            send_sem=send_sem.at[number[0]],
+            recv_sem=recv_sem.at[number[1]],
             device_id=peer(steps),
             device_id_type=MESH,
         )
@@ -183,37 +191,64 @@
             def _():
                 land[...] = jnp.zeros(land.shape, F32)
 
-    g_pos = both("gx", mine.at[1], theirs.at[0], mine.at[0], theirs.at[1])
-    g_y = both("gy", y_out.at[1], yb.at[:, 0:8], y_out.at[0], yb.at[:, 16:24])
-    g_z = both("gz", z_out.at[1], z_in.at[0:8], z_out.at[0], z_in.at[8:16])
-    g_yz = diagonal(("gy", "gz"), lambda y, z: z_out.at[z], yz_in)
-    g_part = both("gx", part_out.at[1], part_in.at[0], part_out.at[0], part_in.at[1])
-    d_terms = both("gx", terms_pack, terms_in.at[0], terms_pack, terms_in.at[1])
+    g_pos = [
+        both(2 * h, "gx", mine.at[1, h], theirs.at[0, h], mine.at[0, h], theirs.at[1, h])
+        for h in range(PARTS)
+    ]
+    first = 2 * PARTS
+    g_y = both(first, "gy", y_out.at[1], yb.at[:, 0:8], y_out.at[0], yb.at[:, 16:24])
+    g_z = both(first + 2, "gz", z_out.at[1], z_in.at[0:8], z_out.at[0], z_in.at[8:16])
+    g_yz = diagonal(first + 4, ("gy", "gz"), lambda y, z: z_out.at[z], yz_in)
+    g_part = [
+        both(
+            first + 20 + 2 * h,
+            "gx",
+            part_out.at[1, h],
+            part_in.at[0, h],
+            part_out.at[0, h],
+            part_in.at[1, h],
+        )
+        for h in range(PARTS)
+    ]
+    d_terms = [
+        both(
+            2 * h,
+            "gx",
+            terms_pack.at[h],
+            terms_in.at[0, h],
+            terms_pack.at[h],
+            terms_in.at[1, h],
+            again=g_pos[h],
+        )
+        for h in range(PARTS)
+    ]
     d_z = both(
+        first + 16,
         "gz",
         dz_out.at[8:16, 0:OWN],
         dz_in.at[0:8],
         dz_out.at[0:8, 0:OWN],
         dz_in.at[8:16],
     )
-    d_y = both("gy", dy.at[16:24], dy_in.at[0], dy.at[0:8], dy_in.at[1])
+    d_y = both(first + 18, "gy", dy.at[16:24], dy_in.at[0], dy.at[0:8], dy_in.at[1])
     d_yz = diagonal(
-        ("gy", "gz"), lambda y, z: dz_out.at[8 * z : 8 * z + 8, OWN:COLS], dyz_in
+        first + 20, ("gy", "gz"), lambda y, z: dz_out.at[8 * z : 8 * z + 8, OWN:COLS], dyz_in
     )
-    d_xz = diagonal(("gx", "gz"), lambda x, z: dxz_out.at[8 * z : 8 * z + 8], dxz_in)
+    d_xz = diagonal(first, ("gx", "gz"), lambda x, z: dxz_out.at[8 * z : 8 * z + 8], dxz_in)
 
     def edge(x, y):
         first = 16 * x + 8 * y
         return slice(first, first + 8)
 
-    d_xy = diagonal(("gx", "gy"), lambda x, y: dxy_out.at[edge(x, y), 0:128], dxy_in)
+    d_xy = diagonal(first + 4, ("gx", "gy"), lambda x, y: dxy_out.at[edge(x, y), 0:128], dxy_in)
     d_xyz = diagonal(
-        ("gx", "gy", "gz"), lambda x, y, z: dxy_out.at[edge(x, y), 128:256], dxyz_in
+        first + 8, ("gx", "gy", "gz"), lambda x, y, z: dxy_out.at[edge(x, y), 128:256], dxyz_in
     )
-    groups = (g_pos, g_y, g_z, g_yz, g_part, d_terms, d_xz, d_xy, d_xyz, d_z, d_y, d_yz)
+    groups = (g_y, g_z, g_yz, d_xz, d_xy, d_xyz, d_z, d_y, d_yz)
+    groups += tuple(g_pos) + tuple(g_part) + tuple(d_terms)
 
     barrier = pltpu.get_barrier_semaphore()
-    for _, steps, _, _ in g_pos + g_y + g_z + g_yz:
+    for _, steps, _, _ in g_pos[0] + g_y + g_z + g_yz:
         pl.when(there(steps))(
             lambda s=steps: pl.semaphore_signal(
                 barrier, inc=1, device_id=peer(s), device_id_type=MESH
@@ -234,7 +269,7 @@
             (diam_hbm, diam),
         )
     ):
-        loads.append(pltpu.make_async_copy(source, land, local_sem.at[number]))
+        loads.append(pltpu.make_async_copy(source, land, send_sem.at[first + 8 + number]))
         loads[-1].start()
 
     for group in groups:
@@ -246,8 +281,6 @@
     zt[:, 10:16] = jnp.zeros((OWN // 128, 6, 128), F32)
     s_hi[OWN + 32 : COLS] = jnp.zeros((96, n), BF16)
     s_lo[OWN + 32 : COLS] = jnp.zeros((96, n), BF16)
-    t_hi[NS * CK + 16 :] = jnp.zeros((112, n), BF16)
-    t_lo[NS * CK + 16 :] = jnp.zeros((112, n), BF16)
 
     for load in loads[0:4]:
         load.wait()
@@ -256,7 +289,8 @@
     reach = [tent(at[0] - (place - cell[0])) for place in (-1.0, float(CI))]
     for x in range(2):
         for number, row in enumerate((reach[x], at[1], cell[1], at[2], cell[2])):
-            pack(mine.at[x], number, row)
+            for h, part in enumerate(parts):
+                pack(mine.at[x, h], number, row[:, part])
 
     for load in loads[4:]:
         load.wait()
@@ -274,32 +308,33 @@
             a_lo[f * CK : f * CK + CK, b * 128 : b * 128 + 128] = lo
     near = {axis: jnp.minimum(me[axis], 1) + jnp.minimum(ends[axis] - me[axis], 1) for axis in axes}
     pl.semaphore_wait(barrier, near["gx"] + near["gy"] + near["gz"] + near["gy"] * near["gz"])
-    send(g_pos)
-
+    for h in range(PARTS):
+        send(g_pos[h])
     send(g_y)
     send(g_z)
     send(g_yz)
 
-    def ramp(rows):
-        return iota((rows, n), 0).astype(F32)
+    def ramp(rows, columns=n):
+        return iota((rows, columns), 0).astype(F32)
 
     row16 = iota((16, n), 0)
 
-    def k_weights(x, offset, cell):
-        hi, lo = split(tent(offset - (ramp(CK) - cell)))
-        l_hi[x, 0:CK] = hi
-        l_lo[x, 0:CK] = lo
+    def k_weights(x, part, offset, cell):
+        rows = iota((16, offset.shape[1]), 0)
+        hi, lo = split(tent(offset - (ramp(CK, offset.shape[1]) - cell)))
+        l_hi[x, 0:CK, part] = hi
+        l_lo[x, 0:CK, part] = lo
         low, high = tent(offset - (-1.0 - cell)), tent(offset - (float(CK) - cell))
-        hi, lo = split(jnp.where(row16 == 0, low, jnp.where(row16 == 8, high, 0.0)))
-        l_hi[x, CK:] = hi
-        l_lo[x, CK:] = lo
+        hi, lo = split(jnp.where(rows == 0, low, jnp.where(rows == 8, high, 0.0)))
+        l_hi[x, CK:, part] = hi
+        l_lo[x, CK:, part] = lo
         return low, high
 
     wi[...] = jnp.where(row16 < CI, tent(at[0] - (ramp(16) - cell[0])), 0.0)
     wj = tent(at[1] - (ramp(CJ) - cell[1]))
     wj_ends = (tent(at[1] - (-1.0 - cell[1])), tent(at[1] - (float(CJ) - cell[1])))
     lines[...] = tent(at[2] - (ramp(CK) - cell[2]))
-    line_ends[0:1], line_ends[1:2] = k_weights(2, at[2], cell[2])
+    line_ends[0:1], line_ends[1:2] = k_weights(2, slice(0, n), at[2], cell[2])
     for i in range(CI):
         hi, lo = split(wi[i : i + 1] * wj)
         s_hi[i * CJ : i * CJ + CJ] = hi
@@ -395,68 +430,76 @@
     for chunk in chunks[:2]:
         gather(chunk)
 
-    arrive(g_pos)
-    for x in range(2):
-        near_x, at_j, cell_j, at_k, cell_k = [unpack(theirs.at[x], q) for q in range(5)]
-        ws[x] = near_x * tent(at_j - (ramp(CJ) - cell_j))
-        ws_ends[x, 0:1] = near_x * tent(at_j - (-1.0 - cell_j))
-        ws_ends[x, 1:2] = near_x * tent(at_j - (float(CJ) - cell_j))
-        k_weights(x, at_k, cell_k)
-    for x in range(2):
-        for chunk in chunks:
-            top, low = l_hi[x, 0:CK, chunk], l_lo[x, 0:CK, chunk]
-            top_z, low_z = l_hi[x, CK:, chunk], l_lo[x, CK:, chunk]
-            right = jnp.concatenate(
-                [top, low, top, top_z, low_z, top_z, jnp.zeros((80, 256), BF16)], axis=0
-            )
-            value = jnp.dot(e_lhs[x], right, preferred_element_type=F32)
-            last = NF * CJ
-            total = value[last : last + 8] * ws_ends[x, 0:1, chunk]
-            total = total + value[last + 8 : last + 16] * ws_ends[x, 1:2, chunk]
-            weight = ws[x, :, chunk]
-            for f in range(NF):
-                row = jnp.sum(value[f * CJ : f * CJ + CJ] * weight, axis=0, keepdims=True)
-                row = row + total[f : f + 1]
-                for b in range(2):
-                    put = f * (n // 128) + chunk.start // 128 + b
-                    part_out[x, put : put + 1, :] = row[:, b * 128 : b * 128 + 128]
-    send(g_part)
+    for h, part in enumerate(parts):
+        arrive(g_pos[h])
+        for x in range(2):
+            near_x, at_j, cell_j, at_k, cell_k = [unpack(theirs.at[x, h], q) for q in range(5)]
+            ws[x, :, part] = near_x * tent(at_j - (ramp(CJ, width) - cell_j))
+            ws_ends[x, 0:1, part] = near_x * tent(at_j - (-1.0 - cell_j))
+            ws_ends[x, 1:2, part] = near_x * tent(at_j - (float(CJ) - cell_j))
+            k_weights(x, part, at_k, cell_k)
+        for x in range(2):
+            for start in range(part.start, part.stop, 256):
+                chunk = slice(start, start + 256)
+                top, low = l_hi[x, 0:CK, chunk], l_lo[x, 0:CK, chunk]
+                top_z, low_z = l_hi[x, CK:, chunk], l_lo[x, CK:, chunk]
+                right = jnp.concatenate(
+                    [top, low, top, top_z, low_z, top_z, jnp.zeros((80, 256), BF16)], axis=0
+                )
+                value = jnp.dot(e_lhs[x], right, preferred_element_type=F32)
+                last = NF * CJ
+                total = value[last : last + 8] * ws_ends[x, 0:1, chunk]
+                total = total + value[last + 8 : last + 16] * ws_ends[x, 1:2, chunk]
+                weight = ws[x, :, chunk]
+                for f in range(NF):
+                    row = jnp.sum(value[f * CJ : f * CJ + CJ] * weight, axis=0, keepdims=True)
+                    row = row + total[f : f + 1]
+                    pack(part_out.at[x, h], f, row, (start - part.start) // 128)
+        send(g_part[h])
 
     for chunk in chunks[2:]:
         gather(chunk)
 
-    motion = mot[...]
-    warmth = heat[...].reshape(1, n)
-    q = diam[...].reshape(1, n)
-    live = iota((1, n), 1) // TILE < tally[0]
-    arrive(g_part)
-    got = [
-        gathered[f : f + 1] + unpack(part_in.at[0], f) + unpack(part_in.at[1], f)
-        for f in range(NF)
-    ]
-    gas = jnp.concatenate(got[0:3], axis=0)
-    gas_heat, moisture, rho = got[3:6]
-    drag = step_time / (0.5 * q)
-    new_motion = (motion + drag * gas) / (1.0 + drag)
-    mass = q * jnp.sqrt(q)
-    vapour = jnp.exp(4.0 * (warmth - 1.0))
-    decay = step_time * evap_rate * rho * (vapour - moisture)
-    new_q = q - decay
-    new_mass = new_q * jnp.sqrt(new_q)
-    conduction = step_time * heat_rate * rho / q
-    new_heat = (warmth + conduction * gas_heat) / (1.0 + conduction) - (
-        boiling_energy_drain * decay / q
-    )
-    state[0:3] = jnp.where(live, new_motion, motion)
-    state[3:4] = jnp.where(live, new_heat, warmth)
-    state[4:5] = jnp.where(live, new_q, q)
-    terms_out[0:3] = jnp.where(live, mass * (motion - new_motion), 0.0)
-    terms_out[3:4] = jnp.where(live, mass * (warmth - new_heat), 0.0)
-    terms_out[4:5] = jnp.where(live, mass - new_mass, 0.0)
+    for group in (*g_pos, g_y, g_z, g_yz):
+        sent(group)
+
     terms_out[5:8] = jnp.zeros((3, n), F32)
-    for c in range(NS):
-        pack(terms_pack, c, terms_out[c : c + 1])
-    send(d_terms)
+    for h, part in enumerate(parts):
+        motion = mot[:, part]
+        warmth = heat[part].reshape(1, width)
+        q = diam[part].reshape(1, width)
+        live = (iota((1, width), 1) + h * width) // TILE < tally[0]
+        arrive(g_part[h])
+        got = [
+            gathered[f : f + 1, part]
+            + unpack(part_in.at[0, h], f)
+            + unpack(part_in.at[1, h], f)
+            for f in range(NF)
+        ]
+        gas = jnp.concatenate(got[0:3], axis=0)
+        gas_heat, moisture, rho = got[3:6]
+        drag = step_time / (0.5 * q)
+        new_motion = (motion + drag * gas) / (1.0 + drag)
+        mass = q * jnp.sqrt(q)
+        vapour = jnp.exp(4.0 * (warmth - 1.0))
+        decay = step_time * evap_rate * rho * (vapour - moisture)
+        new_q = q - decay
+        new_mass = new_q * jnp.sqrt(new_q)
+        conduction = step_time * heat_rate * rho / q
+        new_heat = (warmth + conduction * gas_heat) / (1.0 + conduction) - (
+            boiling_energy_drain * decay / q
+        )
+        state[0:3, part] = jnp.where(live, new_motion, motion)
+        state[3:4, part] = jnp.where(live, new_heat, warmth)
+        state[4:5, part] = jnp.where(live, new_q, q)
+        pushes = jnp.where(live, mass * (motion - new_motion), 0.0)
+        terms = [pushes[c : c + 1] for c in range(3)]
+        terms.append(jnp.where(live, mass * (warmth - new_heat), 0.0))
+        terms.append(jnp.where(live, mass - new_mass, 0.0))
+        for c in range(NS):
+            terms_out[c : c + 1, part] = terms[c]
+            pack(terms_pack.at[h], c, terms[c])
+        send(d_terms[h])
 
     def cross(left, right):
         return lax.dot_general(
@@ -467,13 +510,10 @@
         [terms_out[...] * line_ends[0:1], terms_out[...] * line_ends[1:2]], axis=0
     )
     hi, lo = split(tail)
-    t_hi[NS * CK : NS * CK + 16] = hi
-    t_lo[NS * CK : NS * CK + 16] = lo
+    tail = jnp.concatenate([hi, hi, lo], axis=1)
+    tail = jnp.concatenate([tail, jnp.zeros((112, 3 * n), BF16)], axis=0)
     left = jnp.concatenate([x_hi[...], x_lo[...], x_hi[...]], axis=1)
-    right = jnp.concatenate(
-        [jnp.concatenate([hi, hi, lo], axis=1), jnp.zeros((112, 3 * n), BF16)], axis=0
-    )
-    dxz_out[...] = cross(left, right).T[0:16]
+    dxz_out[...] = cross(left, tail).T[0:16]
     hi, lo = split(
         jnp.concatenate([terms_out[...] * edges[line : line + 1] for line in range(4)], axis=0)
     )
@@ -486,19 +526,25 @@
     send(d_xy)
     send(d_xz)
 
-    for c in range(NS):
-        hi, lo = split(terms_out[c : c + 1] * lines[...])
-        t_hi[c * CK : c * CK + CK] = hi
-        t_lo[c * CK : c * CK + CK] = lo
-
     lines_used = slice(0, OWN + 32)
-    for w in range(3):
-        column = slice(w * 256, w * 256 + 256)
+    for w in (2, 0, 1):
         left = jnp.concatenate(
             [s_hi[lines_used], s_lo[lines_used], s_hi[lines_used]], axis=1
         )
-        right = jnp.concatenate([t_hi[column], t_hi[column], t_lo[column]], axis=1)
-        value = cross(left, right)
+        right = []
+        for c in (2 * w, 2 * w + 1):
+            if c < NS:
+                hi, lo = split(terms_out[c : c + 1] * lines[...])
+                right.append(jnp.concatenate([hi, hi, lo], axis=1))
+            else:
+                right.append(tail)
+        right = jnp.concatenate(right, axis=0)
+        if w < 2:
+            value = cross(left, right)
+        else:
+            value = jnp.concatenate(
+                [cross(left[0:272], right), cross(left[272:], right)], axis=0
+            )
         for h in range(2):
             c = 2 * w + h
             half = value[:, h * 128 : h * 128 + 128]
@@ -511,27 +557,29 @@
                 rest = jnp.concatenate([half[OWN : OWN + 32], jnp.zeros((96, 128), F32)], axis=0)
                 dz_out[:, OWN:COLS] = rest.T[0:16]
 
+    for group in g_part:
+        sent(group)
     send(d_z)
     send(d_yz)
     send(d_y)
 
-    for group in (g_pos, g_y, g_z, g_yz, g_part):
-        sent(group)
-    arrive(d_terms)
-    for x in range(2):
-        i = 0 if x == 0 else CI - 1
-        weight = ws[x]
-        for c in range(NS):
-            hi, lo = split(unpack(terms_in.at[x], c) * weight)
-            u_hi[x, c * CJ : c * CJ + CJ] = hi
-            u_lo[x, c * CJ : c * CJ + CJ] = lo
-        left = jnp.concatenate([u_hi[x], u_hi[x], u_lo[x]], axis=1)
-        right = jnp.concatenate([l_hi[x, 0:CK], l_lo[x, 0:CK], l_hi[x, 0:CK]], axis=1)
-        value = cross(left, right)
-        for c in range(NS):
-            out[c, i] = out[c, i] + value[c * CJ : c * CJ + CJ]
-
-    for group in (d_terms, d_xz, d_xy, d_xyz):
+    for h, part in enumerate(parts):
+        arrive(d_terms[h])
+        for x in range(2):
+            i = 0 if x == 0 else CI - 1
+            weight = ws[x, :, part]
+            left = []
+            for c in range(NS):
+                hi, lo = split(unpack(terms_in.at[x, h], c) * weight)
+                left.append(jnp.concatenate([hi, hi, lo], axis=1))
+            left = jnp.concatenate(left, axis=0)
+            hi, lo = l_hi[x, 0:CK, part], l_lo[x, 0:CK, part]
+            right = jnp.concatenate([hi, lo, hi], axis=1)
+            value = cross(left, right)
+            for c in range(NS):
+                out[c, i] = out[c, i] + value[c * CJ : c * CJ + CJ]
+
+    for group in (*d_terms, d_xz, d_xy, d_xyz):
         sent(group)
     arrive(d_z)
     arrive(d_y)
@@ -628,19 +676,15 @@
             pltpu.VMEM((n,), jnp.int32),
             pltpu.VMEM((n,), jnp.int32),
             pltpu.VMEM((n,), jnp.int32),
-            pltpu.VMEM((2, 5 * n // 128, 128), F32),
-            pltpu.VMEM((2, 5 * n // 128, 128), F32),
+            pltpu.VMEM((2, PARTS, 5 * n // PARTS // 128, 128), F32),
+            pltpu.VMEM((2, PARTS, 5 * n // PARTS // 128, 128), F32),
             pltpu.VMEM((ROWS, COLS), BF16),
             pltpu.VMEM((ROWS, COLS), BF16),
             pltpu.VMEM((COLS, n), BF16),
             pltpu.VMEM((COLS, n), BF16),
-            pltpu.VMEM((768, n), BF16),
-            pltpu.VMEM((768, n), BF16),
             pltpu.VMEM((2, planes, 512), BF16),
             pltpu.VMEM((3, CK + 16, n), BF16),
             pltpu.VMEM((3, CK + 16, n), BF16),
-            pltpu.VMEM((2, NS * CJ, n), BF16),
-            pltpu.VMEM((2, NS * CJ, n), BF16),
             pltpu.VMEM((2 * CJ, n), BF16),
             pltpu.VMEM((2 * CJ, n), BF16),
             pltpu.VMEM((8, n), F32),
@@ -650,11 +694,11 @@
             pltpu.VMEM((CK, n), F32),
             pltpu.VMEM((8, n), F32),
             pltpu.VMEM((8, n), F32),
-            pltpu.VMEM((2, NF * n // 128, 128), F32),
-            pltpu.VMEM((2, NF * n // 128, 128), F32),
+            pltpu.VMEM((2, PARTS, NF * n // PARTS // 128, 128), F32),
+            pltpu.VMEM((2, PARTS, NF * n // PARTS // 128, 128), F32),
             pltpu.VMEM((8, n), F32),
-            pltpu.VMEM((NS * n // 128, 128), F32),
-            pltpu.VMEM((2, NS * n // 128, 128), F32),
+            pltpu.VMEM((PARTS, NS * n // PARTS // 128, 128), F32),
+            pltpu.VMEM((2, PARTS, NS * n // PARTS // 128, 128), F32),
             pltpu.VMEM((NF, 128, CK), F32),
             pltpu.VMEM((2, NF, 8, CK), F32),
             pltpu.VMEM((2, 8, OWN), F32),
@@ -670,9 +714,8 @@
             pltpu.VMEM((32, 256), F32),
             pltpu.VMEM((2, 2, 8, 128), F32),
             pltpu.VMEM((2, 2, 2, 8, 128), F32),
-            pltpu.SemaphoreType.DMA((9,)),
-            pltpu.SemaphoreType.DMA((38,)),
-            pltpu.SemaphoreType.DMA((38,)),
+            pltpu.SemaphoreType.DMA((2 * PARTS + 20 + max(4, 2 * PARTS),)),
+            pltpu.SemaphoreType.DMA((32 + 4 * PARTS,)),
         ],
         compiler_params=pltpu.CompilerParams(
             collective_id=0, has_side_effects=True, vmem_limit_bytes=32 * 1024 * 1024

time: 27.9 us -> 27.2 us (0.975)
  Pallas kernels: 26.5 us -> 25.7 us
    pallas_call x1, Pallas kernels: 25.1 us -> 24.4 us  [local(): pl.pallas_call(functools.partial(kernel, sizes), out_shape=(jax.ShapeDtyp...]
where the time goes in v5:
time: 27.2 us; the launch traced here: 27 us
  Pallas kernels  25.7 us (94%)
  between operations  1.29 us (5%)
    pallas_call x1, Pallas kernels, local(): pl.pallas_call(functools.partial(kernel, sizes), out_shape=(jax.ShapeDtyp...  24.4 us
    pallas_call x1, Pallas kernels, local(): pl.pallas_call(deliver, out_shape=tuple((jax.ShapeDtypeStruct(part.shape,...  1.34 us

profile of v5, /device:TPU:71, one launch (start us, length us, event | category | flops | bytes accessed | tf_op | source)
XLA Modules:
  0.0 27.0 jit_solution(2473765409605689346)
XLA Ops:
  1.3 24.4 %shard_map.113 = (f32[5,8,64,128]{3,2,1,0:T(8,128)S(1)}, f32[5,1024]{1,0:T(8,128)S(1)}, f32[4,16,128]{2,1,0:T(8,128)S(1)}, f32[2,8,640]{2,1,0:T(8,128)S(1)}) custom-call(f32[3,8,64,128]{3,2,1,0:T(8,128)} %vel.1, f32[3,8,64,128]{3,2,1,0:T(8,128)} %scal.1, f32[3,1024]{1,0:T(4,128)} %pos_hbm.1, f32[3,1024]{1,0:T(4,128)} %mot_hbm.1, f32[1024]{0:T(1024)} %heat_hbm.1, ...), custom_call_target="tpu_custom_call" | custom-call | tf_op jit(solution)/shard_map/pallas_call | solution.py:660
  25.7 1.3 %shard_map.114 = (f32[5,8,64,128]{3,2,1,0:T(8,128)}, f32[5,1024]{1,0:T(8,128)}) custom-call(f32[5,8,64,128]{3,2,1,0:T(8,128)S(1)} %get-tuple-element.6.part, f32[5,1024]{1,0:T(8,128)S(1)} %get-tuple-element.7.state, f32[4,16,128]{2,1,0:T(8,128)S(1)} %get-tuple-element.8.zt, f32[2,8,640]{2,1,0:T(8,128)S(1)} %get-tuple-element.9.rows), custom_call_target="tpu_custom_call" | custom-call | tf_op jit(solution)/shard_map/pallas_call | solution.py:724

commit v6 on v5

--- a/solution.py
+++ b/solution.py
@@ -15,7 +15,7 @@
 OWN = CI * CJ
 COLS = OWN + 128
 ROWS = NF * CK + 16
-PARTS = 1
+PARTS = 2
 MESH = pl.DeviceIdType.MESH
 F32 = jnp.float32
 BF16 = jnp.bfloat16
@@ -50,7 +50,7 @@
     li_hbm,
     lj_hbm,
     lk_hbm,
-    tally,
+    tally_hbm,
     out,
     state,
     zt,
@@ -63,6 +63,7 @@
     li,
     lj,
     lk,
+    tally,
     mine,
     theirs,
     a_hi,
@@ -267,6 +268,7 @@
             (mot_hbm, mot),
             (heat_hbm, heat),
             (diam_hbm, diam),
+            (tally_hbm, tally),
         )
     ):
         loads.append(pltpu.make_async_copy(source, land, send_sem.at[first + 8 + number]))
@@ -665,7 +667,7 @@
             jax.ShapeDtypeStruct((OWN // 128, 16, 128), F32),
             jax.ShapeDtypeStruct((2, 8, NS * CK), F32),
         ),
-        in_specs=[hbm] * 9 + [pl.BlockSpec(memory_space=pltpu.SMEM)],
+        in_specs=[hbm] * 9 + [pl.BlockSpec(memory_space=pl.ANY)],
         out_specs=(vmem,) * 4,
         scratch_shapes=[
             pltpu.VMEM((NF, CI, CJ, CK), F32),
@@ -676,6 +678,7 @@
             pltpu.VMEM((n,), jnp.int32),
             pltpu.VMEM((n,), jnp.int32),
             pltpu.VMEM((n,), jnp.int32),
+            pltpu.SMEM((1,), jnp.int32),
             pltpu.VMEM((2, PARTS, 5 * n // PARTS // 128, 128), F32),
             pltpu.VMEM((2, PARTS, 5 * n // PARTS // 128, 128), F32),
             pltpu.VMEM((ROWS, COLS), BF16),

time: 27.2 us -> 27 us (level)
  no operation moved by 1% of the time
where the time goes in v6:
time: 27 us; the launch traced here: 26.8 us
  Pallas kernels  25.5 us (94%)
  between operations  1.29 us (5%)
    pallas_call x1, Pallas kernels, local(): pl.pallas_call(functools.partial(kernel, sizes), out_shape=(jax.ShapeDtyp...  24.2 us
    pallas_call x1, Pallas kernels, local(): pl.pallas_call(deliver, out_shape=tuple((jax.ShapeDtypeStruct(part.shape,...  1.34 us

profile of v6, /device:TPU:71, one launch (start us, length us, event | category | flops | bytes accessed | tf_op | source)
XLA Modules:
  0.0 26.8 jit_solution(17029336255390069576)
XLA Ops:
  1.3 24.2 %shard_map.113 = (f32[5,8,64,128]{3,2,1,0:T(8,128)S(1)}, f32[5,1024]{1,0:T(8,128)S(1)}, f32[4,16,128]{2,1,0:T(8,128)S(1)}, f32[2,8,640]{2,1,0:T(8,128)S(1)}) custom-call(f32[3,8,64,128]{3,2,1,0:T(8,128)} %vel.1, f32[3,8,64,128]{3,2,1,0:T(8,128)} %scal.1, f32[3,1024]{1,0:T(4,128)} %pos_hbm.1, f32[3,1024]{1,0:T(4,128)} %mot_hbm.1, f32[1024]{0:T(1024)} %heat_hbm.1, ...), custom_call_target="tpu_custom_call" | custom-call | tf_op jit(solution)/shard_map/pallas_call | solution.py:662
  25.4 1.3 %shard_map.114 = (f32[5,8,64,128]{3,2,1,0:T(8,128)}, f32[5,1024]{1,0:T(8,128)}) custom-call(f32[5,8,64,128]{3,2,1,0:T(8,128)S(1)} %get-tuple-element.6.part, f32[5,1024]{1,0:T(8,128)S(1)} %get-tuple-element.7.state, f32[4,16,128]{2,1,0:T(8,128)S(1)} %get-tuple-element.8.zt, f32[2,8,640]{2,1,0:T(8,128)S(1)} %get-tuple-element.9.rows), custom_call_target="tpu_custom_call" | custom-call | tf_op jit(solution)/shard_map/pallas_call | solution.py:727

commit v7 on v6

--- a/solution.py
+++ b/solution.py
@@ -429,9 +429,6 @@
                 total = total + value[row : row + 1] * line_ends[z : z + 1, chunk]
             gathered[f : f + 1, chunk] = total
 
-    for chunk in chunks[:2]:
-        gather(chunk)
-
     for h, part in enumerate(parts):
         arrive(g_pos[h])
         for x in range(2):
@@ -459,7 +456,7 @@
                     pack(part_out.at[x, h], f, row, (start - part.start) // 128)
         send(g_part[h])
 
-    for chunk in chunks[2:]:
+    for chunk in chunks:
         gather(chunk)
 
     for group in (*g_pos, g_y, g_z, g_yz):

time: 27 us -> 26.5 us (0.981)
  Pallas kernels: 25.5 us -> 25 us
    pallas_call x1, Pallas kernels: 24.2 us -> 23.7 us  [local(): pl.pallas_call(functools.partial(kernel, sizes), out_shape=(jax.ShapeDtyp...]
where the time goes in v7:
time: 26.5 us; the launch traced here: 26.3 us
  Pallas kernels  25 us (94%)
  between operations  1.29 us (5%)
    pallas_call x1, Pallas kernels, local(): pl.pallas_call(functools.partial(kernel, sizes), out_shape=(jax.ShapeDtyp...  23.7 us
    pallas_call x1, Pallas kernels, local(): pl.pallas_call(deliver, out_shape=tuple((jax.ShapeDtypeStruct(part.shape,...  1.34 us

profile of v7, /device:TPU:71, one launch (start us, length us, event | category | flops | bytes accessed | tf_op | source)
XLA Modules:
  0.0 26.3 jit_solution(1892056228046196920)
XLA Ops:
  1.3 23.7 %shard_map.113 = (f32[5,8,64,128]{3,2,1,0:T(8,128)S(1)}, f32[5,1024]{1,0:T(8,128)S(1)}, f32[4,16,128]{2,1,0:T(8,128)S(1)}, f32[2,8,640]{2,1,0:T(8,128)S(1)}) custom-call(f32[3,8,64,128]{3,2,1,0:T(8,128)} %vel.1, f32[3,8,64,128]{3,2,1,0:T(8,128)} %scal.1, f32[3,1024]{1,0:T(4,128)} %pos_hbm.1, f32[3,1024]{1,0:T(4,128)} %mot_hbm.1, f32[1024]{0:T(1024)} %heat_hbm.1, ...), custom_call_target="tpu_custom_call" | custom-call | tf_op jit(solution)/shard_map/pallas_call | solution.py:659
  25.0 1.3 %shard_map.114 = (f32[5,8,64,128]{3,2,1,0:T(8,128)}, f32[5,1024]{1,0:T(8,128)}) custom-call(f32[5,8,64,128]{3,2,1,0:T(8,128)S(1)} %get-tuple-element.6.part, f32[5,1024]{1,0:T(8,128)S(1)} %get-tuple-element.7.state, f32[4,16,128]{2,1,0:T(8,128)S(1)} %get-tuple-element.8.zt, f32[2,8,640]{2,1,0:T(8,128)S(1)} %get-tuple-element.9.rows), custom_call_target="tpu_custom_call" | custom-call | tf_op jit(solution)/shard_map/pallas_call | solution.py:724
